TPU v7x, 256 devices: a whole 4x4x8 slice. The times are simulated.
256 devices in a mesh: pb: 64 (over x, y, z_hi, core), ga: 4 (over z_lo).
Axes of the slice: x: 4, y: 4, z: 8 (z_hi: 2, z_lo: 4; z = z_hi * 4 + z_lo), core: 2. Of those that a mesh axis runs over, the one named last changes fastest.
Arguments:
- query_points: float32 [3, 262144], P(None, 'pb'), may hold values from 0 to 1
- cotangent: bfloat16 [64, 262144], P(None, 'pb'), may hold values from -6 to 6
- slab_ids: int32 [8, 262144], P(None, 'pb'), may hold values from -1 to 3
- rel_cells: int32 [8, 262144], P(None, 'pb'), may hold values from 0 to 511
- offsets: int32 [4, 2048], P('ga', 'pb'), may hold values from 0 to 15872
- latent: bfloat16 [4, 64, 16384], P('ga', None, 'pb'), may hold values from -6 to 6
- w_in: float32 [80, 6], replicated, may hold values from -2.5 to 2.5
- b_in: float32 [80], replicated, may hold values from -3 to 3
- w_out: bfloat16 [64, 80], replicated, may hold values from -0.625 to 0.625
- b_out: float32 [64], replicated, may hold values from -3 to 3
Outputs:
- grid_grad: float32 [4, 64, 16384], P('ga', None, 'pb')
- w_in_grad: float32 [80, 6], replicated
- b_in_grad: float32 [80], replicated
- w_out_grad: float32 [64, 80], replicated
- b_out_grad: float32 [64], replicated
Inputs may be any that keep to these rules, and one draw needn't show every extreme that they name: `slab_ids`: -1 marks a padding slot; otherwise the slab that holds the neighbour cell.
All inputs are finite; a program needn't handle non-finite values.
Results may differ from a plain program's by a relative error of at most 0.0085.
Values may be sent and summed in bfloat16 or wider, within the bound.
A program may use at most 64 MiB of HBM per device.

v0:
```python
import functools
import math

import jax
import jax.numpy as jnp
from jax import lax
from jax.sharding import Mesh
from jax.sharding import PartitionSpec as P

KN = 8
TILE = 128
WIN = 512
GX = 64
ZS = 4
PB = ("pb_0", "pb_1", "pb_2", "pb_3")
PB_GA = ("pb_0", "pb_1", "pb_2", "pb_3", "ga")


def cut_along(value, dim, length):
    before, after = (value.shape[:dim], value.shape[dim + 1 :])
    return jnp.moveaxis(value.reshape(*before, length, -1, *after), dim, 0)


def sum_at_owner(value, axis, dim):
    tiles = cut_along(value, dim, lax.axis_size(axis))
    arrived = lax.all_to_all(tiles, axis, split_axis=0, concat_axis=0, tiled=True)
    return arrived.astype(jnp.float32).sum(axis=0)


def by_axis(value, axes):
    return functools.reduce(lax.psum, axes, value)


def gelu_exact(values):
    return jax.nn.gelu(values, approximate=False)


def shards(query_points, cotangent, slab_ids, rel_cells, offsets, latent, w_in, b_in, w_out, b_out):
    channels = latent.shape[1]
    slab_feats = lax.all_gather(latent, PB, axis=2, tiled=True)[0]
    cells_slab = slab_feats.shape[1]
    slab_here = lax.axis_index("ga")
    queries_dev = query_points.shape[1]
    tiles_dev = queries_dev // TILE
    per_block = math.gcd(tiles_dev, 4)
    blocks = tiles_dev // per_block
    entries = KN * TILE

    def reshape_tiles(values):
        leading = values.shape[0]
        return values.reshape(leading, blocks, per_block, TILE).transpose(1, 2, 0, 3)

    def tile_work(anchor, points, cot_cols, slabs, rels):
        window = lax.dynamic_slice_in_dim(slab_feats, anchor, WIN, 1)
        rel_flat = rels.reshape(-1)
        live_flat = slabs.reshape(-1) == slab_here
        onehot = (
            (lax.broadcasted_iota(jnp.int32, (WIN, entries), 0) == rel_flat[None, :])
            & live_flat[None, :]
        ).astype(jnp.bfloat16)
        feats = jnp.dot(window, onehot, preferred_element_type=jnp.float32)
        cell = anchor + rel_flat
        along_x = cell // (GX * ZS)
        along_y = cell // ZS % GX
        along_z = cell % ZS + slab_here * ZS
        centres = jnp.stack(
            [
                (along_x.astype(jnp.float32) + 0.5) / GX,
                (along_y.astype(jnp.float32) + 0.5) / GX,
                (along_z.astype(jnp.float32) + 0.5) / GX,
            ],
            0,
        )
        features_in = jnp.concatenate([jnp.tile(points, (1, KN)), centres], 0)
        mask_flat = live_flat.astype(jnp.float32)
        cot_flat = jnp.tile(cot_cols.astype(jnp.float32), (1, KN))
        preact = (
            jnp.dot(
                w_in,
                features_in,
                precision=lax.Precision.HIGHEST,
                preferred_element_type=jnp.float32,
            )
            + b_in[:, None]
        )
        hidden = gelu_exact(preact).astype(jnp.bfloat16)
        kernel = jnp.dot(w_out, hidden, preferred_element_type=jnp.float32) + b_out[:, None]
        grad_cell = (kernel * cot_flat * mask_flat).astype(jnp.bfloat16)
        grad_kernel = (feats * cot_flat * mask_flat).astype(jnp.bfloat16)
        window_grad = lax.dot_general(
            grad_cell, onehot, (((1,), (1,)), ((), ())), preferred_element_type=jnp.float32
        )
        grad_w_out = lax.dot_general(
            grad_kernel, hidden, (((1,), (1,)), ((), ())), preferred_element_type=jnp.float32
        )
        grad_b_out = jnp.sum(grad_kernel.astype(jnp.float32), 1)
        grad_hidden = lax.dot_general(
            w_out, grad_kernel, (((0,), (0,)), ((), ())), preferred_element_type=jnp.float32
        )
        grad_pre = jax.vjp(gelu_exact, preact)[1](grad_hidden)[0]
        grad_w_in = lax.dot_general(
            grad_pre,
            features_in,
            (((1,), (1,)), ((), ())),
            precision=lax.Precision.HIGHEST,
            preferred_element_type=jnp.float32,
        )
        grad_b_in = jnp.sum(grad_pre, 1)
        return (window_grad, grad_w_in, grad_b_in, grad_w_out, grad_b_out)

    def advance(running, inputs_block):
        partial_grad, totals = running
        anchors, points, cot_cols, slabs, rels = inputs_block
        results = jax.vmap(tile_work)(anchors, points, cot_cols, slabs, rels)
        for number in range(per_block):
            current = lax.dynamic_slice_in_dim(partial_grad, anchors[number], WIN, 1)
            partial_grad = lax.dynamic_update_slice_in_dim(
                partial_grad, current + results[0][number], anchors[number], 1
            )
        totals = tuple((old + jnp.sum(new, 0) for old, new in zip(totals, results[1:])))
        return ((partial_grad, totals), None)

    start_totals = (
        jnp.zeros((w_in.shape[0], 6), jnp.float32),
        jnp.zeros((w_in.shape[0],), jnp.float32),
        jnp.zeros((channels, w_in.shape[0]), jnp.float32),
        jnp.zeros((channels,), jnp.float32),
    )
    start_grid = jnp.zeros((channels, cells_slab), jnp.float32)
    inputs_all = (
        offsets[0].reshape(blocks, per_block),
        reshape_tiles(query_points),
        reshape_tiles(cotangent),
        reshape_tiles(slab_ids),
        reshape_tiles(rel_cells),
    )
    (partial_grad, totals), _ = lax.scan(advance, (start_grid, start_totals), inputs_all)
    owned = sum_at_owner(partial_grad.astype(jnp.bfloat16), PB, 1)
    sums = (
        by_axis(totals[0], PB_GA),
        by_axis(totals[1], PB_GA),
        by_axis(totals[2], PB_GA),
        by_axis(totals[3], PB_GA),
    )
    scale = float(queries_dev * lax.axis_size(PB)) ** (-0.5)
    return (owned[None], sums[0] * scale, sums[1] * scale, sums[2] * scale, sums[3] * scale)


def solution(mesh):
    finer = Mesh(
        mesh.devices.reshape(4, 4, 2, 2, mesh.shape["ga"]), ("pb_0", "pb_1", "pb_2", "pb_3", "ga")
    )
    in_specs = (
        P(None, PB),
        P(None, PB),
        P(None, PB),
        P(None, PB),
        P("ga", PB),
        P("ga", None, PB),
        P(),
        P(),
        P(),
        P(),
    )
    out_specs = (P("ga", None, PB), P(), P(), P(), P())
    return jax.shard_map(
        shards, mesh=finer, in_specs=in_specs, out_specs=out_specs, check_vma=False
    )
```

profile of v0, /device:TPU:1, one launch (start us, length us, event | category | flops | bytes accessed | tf_op | source)
XLA Modules:
  0.0 574.6 jit_solution(1907002252681811050)
XLA Ops:
  10.7 2.3 reshape.397
  13.0 88.5 %all-gather.2.cloned.1.call-done = bf16[1,64,16384]{2,1,0:T(8,128)(2,1)} async-done(((bf16[1,64,256]{2,1,0:T(8,128)(2,1)}), bf16[1,64,16384]{2,1,0:T(8,128)(2,1)}) %all-gather.2.cloned.1.call-update) | async-done | bytes 2097168 | tf_op jit(solution)/shard_map/all_gather | solution.py:40
  101.6 2.3 broadcast_in_dim.12
  103.8 365.0 %while.26 = (s32[]{:T(128)}, f32[64,16384]{1,0:T(8,128)}, f32[80,6]{0,1:T(8,128)S(1)}, f32[80]{0:T(128)S(1)}, f32[64,80]{1,0:T(8,128)S(1)}, /*index=5*/f32[64]{0...) while((s32[]{:T(128)}, f32[64,16384]{1,0:T(8,128)}, ...), condition=%wide.region_3.4_spmd.clone, body=%wide.region_0.3_spmd.clone.sunk | while | flops 747289728 | bytes 21654660 | solution.py:137
  114.8 8.9 %while.27 = (s32[]{:T(128)}, bf16[64,16384]{1,0:T(8,128)(2,1)}, s32[4,2]{0,1:T(2,128)S(1)}, bf16[4,64,512]{2,1,0:T(8,128)(2,1)S(1)}, s32[]{:T(128)}) while((s32[]{:T(128)}, bf16[64,16384]{1,0:T(8,128)(2,1)}, s32[4,2]{0,1:T(2,128)S(1)}, bf16[4,64,512]{2,1,0:T(8,128)(2,1)S(1)}, s32[]{:T(128)}) %tuple.83), condition=%wide.while_cond, body=%wide.while_body.sunk | while | flops 2 | bytes 131177 | solution.py:54
  124.0 2.2 convert_reduce_fusion.3
  126.2 5.4 fusion.121
  131.6 2.3 fusion.122
  133.9 2.6 fusion.128
  160.4 8.9 %while.27 = (s32[]{:T(128)}, bf16[64,16384]{1,0:T(8,128)(2,1)}, s32[4,2]{0,1:T(2,128)S(1)}, bf16[4,64,512]{2,1,0:T(8,128)(2,1)S(1)}, s32[]{:T(128)}) while((s32[]{:T(128)}, bf16[64,16384]{1,0:T(8,128)(2,1)}, s32[4,2]{0,1:T(2,128)S(1)}, bf16[4,64,512]{2,1,0:T(8,128)(2,1)S(1)}, s32[]{:T(128)}) %tuple.83), condition=%wide.while_cond, body=%wide.while_body.sunk | while | flops 2 | bytes 131177 | solution.py:54
  169.6 2.2 convert_reduce_fusion.3
  171.8 5.4 fusion.121
  177.2 2.3 fusion.122
  179.5 2.6 fusion.128
  206.1 8.9 %while.27 = (s32[]{:T(128)}, bf16[64,16384]{1,0:T(8,128)(2,1)}, s32[4,2]{0,1:T(2,128)S(1)}, bf16[4,64,512]{2,1,0:T(8,128)(2,1)S(1)}, s32[]{:T(128)}) while((s32[]{:T(128)}, bf16[64,16384]{1,0:T(8,128)(2,1)}, s32[4,2]{0,1:T(2,128)S(1)}, bf16[4,64,512]{2,1,0:T(8,128)(2,1)S(1)}, s32[]{:T(128)}) %tuple.83), condition=%wide.while_cond, body=%wide.while_body.sunk | while | flops 2 | bytes 131177 | solution.py:54
  217.5 5.4 fusion.121
  222.9 2.3 fusion.122
  225.2 2.6 fusion.128
  251.7 8.9 %while.27 = (s32[]{:T(128)}, bf16[64,16384]{1,0:T(8,128)(2,1)}, s32[4,2]{0,1:T(2,128)S(1)}, bf16[4,64,512]{2,1,0:T(8,128)(2,1)S(1)}, s32[]{:T(128)}) while((s32[]{:T(128)}, bf16[64,16384]{1,0:T(8,128)(2,1)}, s32[4,2]{0,1:T(2,128)S(1)}, bf16[4,64,512]{2,1,0:T(8,128)(2,1)S(1)}, s32[]{:T(128)}) %tuple.83), condition=%wide.while_cond, body=%wide.while_body.sunk | while | flops 2 | bytes 131177 | solution.py:54
  260.9 2.2 convert_reduce_fusion.3
  263.1 5.4 fusion.121
  268.4 2.3 fusion.122
  270.7 2.6 fusion.128
  297.3 8.9 %while.27 = (s32[]{:T(128)}, bf16[64,16384]{1,0:T(8,128)(2,1)}, s32[4,2]{0,1:T(2,128)S(1)}, bf16[4,64,512]{2,1,0:T(8,128)(2,1)S(1)}, s32[]{:T(128)}) while((s32[]{:T(128)}, bf16[64,16384]{1,0:T(8,128)(2,1)}, s32[4,2]{0,1:T(2,128)S(1)}, bf16[4,64,512]{2,1,0:T(8,128)(2,1)S(1)}, s32[]{:T(128)}) %tuple.83), condition=%wide.while_cond, body=%wide.while_body.sunk | while | flops 2 | bytes 131177 | solution.py:54
  308.7 5.4 fusion.121
  314.1 2.3 fusion.122
  316.4 2.6 fusion.128
  342.9 8.9 %while.27 = (s32[]{:T(128)}, bf16[64,16384]{1,0:T(8,128)(2,1)}, s32[4,2]{0,1:T(2,128)S(1)}, bf16[4,64,512]{2,1,0:T(8,128)(2,1)S(1)}, s32[]{:T(128)}) while((s32[]{:T(128)}, bf16[64,16384]{1,0:T(8,128)(2,1)}, s32[4,2]{0,1:T(2,128)S(1)}, bf16[4,64,512]{2,1,0:T(8,128)(2,1)S(1)}, s32[]{:T(128)}) %tuple.83), condition=%wide.while_cond, body=%wide.while_body.sunk | while | flops 2 | bytes 131177 | solution.py:54
  354.3 5.4 fusion.121
  359.7 2.3 fusion.122
  362.0 2.6 fusion.128
  388.6 8.9 %while.27 = (s32[]{:T(128)}, bf16[64,16384]{1,0:T(8,128)(2,1)}, s32[4,2]{0,1:T(2,128)S(1)}, bf16[4,64,512]{2,1,0:T(8,128)(2,1)S(1)}, s32[]{:T(128)}) while((s32[]{:T(128)}, bf16[64,16384]{1,0:T(8,128)(2,1)}, s32[4,2]{0,1:T(2,128)S(1)}, bf16[4,64,512]{2,1,0:T(8,128)(2,1)S(1)}, s32[]{:T(128)}) %tuple.83), condition=%wide.while_cond, body=%wide.while_body.sunk | while | flops 2 | bytes 131177 | solution.py:54
  397.7 2.2 convert_reduce_fusion.3
  400.0 5.4 fusion.121
  405.3 2.3 fusion.122
  407.6 2.6 fusion.128
  434.2 8.9 %while.27 = (s32[]{:T(128)}, bf16[64,16384]{1,0:T(8,128)(2,1)}, s32[4,2]{0,1:T(2,128)S(1)}, bf16[4,64,512]{2,1,0:T(8,128)(2,1)S(1)}, s32[]{:T(128)}) while((s32[]{:T(128)}, bf16[64,16384]{1,0:T(8,128)(2,1)}, s32[4,2]{0,1:T(2,128)S(1)}, bf16[4,64,512]{2,1,0:T(8,128)(2,1)S(1)}, s32[]{:T(128)}) %tuple.83), condition=%wide.while_cond, body=%wide.while_body.sunk | while | flops 2 | bytes 131177 | solution.py:54
  445.6 5.4 fusion.121
  451.0 2.3 fusion.122
  453.3 2.6 fusion.128
  468.9 2.4 convert_element_type.102
  471.8 2.5 copy.31
  474.4 5.2 all-to-all-start
  479.6 28.2 %all-reduce.3 = (f32[80,6]{0,1:T(8,128)S(1)}, f32[80]{0:T(128)S(1)}, f32[64,80]{1,0:T(8,128)S(1)}, f32[64]{0:T(128)S(1)}) all-reduce(f32[80,6]{0,1:T(8,128)S(1)} %get-tuple-element.285, f32[80]{0:T(128)S(1)} %get-tuple-element.286, ...), channel_id=1, replica_groups=mesh['pb_0'=4,'pb_1'=4,'pb_2'=2,'pb_3'=2,'ga'=4] {'pb_0'}, use_global_device_ids=true, to_apply=%region_5.6 | all-reduce | flops 5744 | bytes 45952 | tf_op jit(solution)/shard_map/psum | solution.py:31
  507.8 14.1 %all-reduce.2 = (f32[80,6]{0,1:T(8,128)S(1)}, f32[80]{0:T(128)S(1)}, f32[64,80]{1,0:T(8,128)S(1)}, f32[64]{0:T(128)S(1)}) all-reduce(f32[80,6]{0,1:T(8,128)S(1)} %get-tuple-element.497, f32[80]{0:T(128)S(1)} %get-tuple-element.498, ...), channel_id=1, replica_groups=mesh['pb_0'=4,'pb_1'=4,'pb_2'=2,'pb_3'=2,'ga'=4] {'pb_1'}, use_global_device_ids=true, to_apply=%region_6.7 | all-reduce | flops 5744 | bytes 45952 | tf_op jit(solution)/shard_map/psum | solution.py:31
  522.0 17.8 %all-reduce.5 = (f32[80,6]{0,1:T(8,128)S(1)}, f32[80]{0:T(128)S(1)}, f32[64,80]{1,0:T(8,128)S(1)}, f32[64]{0:T(128)S(1)}) all-reduce(f32[80,6]{0,1:T(8,128)S(1)} %get-tuple-element.493, f32[80]{0:T(128)S(1)} %get-tuple-element.494, ...), channel_id=1, replica_groups=mesh['pb_0'=4,'pb_1'=4,'pb_2'=2,'pb_3'=2,'ga'=4] {'pb_2'}, use_global_device_ids=true, to_apply=%region_7.8 | all-reduce | flops 5744 | bytes 45952 | tf_op jit(solution)/shard_map/psum | solution.py:31
  539.7 12.1 %all-reduce.4 = (f32[80,6]{0,1:T(8,128)S(1)}, f32[80]{0:T(128)S(1)}, f32[64,80]{1,0:T(8,128)S(1)}, f32[64]{0:T(128)S(1)}) all-reduce(f32[80,6]{0,1:T(8,128)S(1)} %get-tuple-element.505, f32[80]{0:T(128)S(1)} %get-tuple-element.506, ...), channel_id=1, replica_groups=mesh['pb_0'=4,'pb_1'=4,'pb_2'=2,'pb_3'=2,'ga'=4] {'pb_3'}, use_global_device_ids=true, to_apply=%region_8.9 | all-reduce | flops 5744 | bytes 45952 | tf_op jit(solution)/shard_map/psum | solution.py:31
  551.8 12.7 %all-reduce.1 = (f32[80,6]{0,1:T(8,128)S(1)}, f32[80]{0:T(128)S(1)}, f32[64,80]{1,0:T(8,128)S(1)}, f32[64]{0:T(128)S(1)}) all-reduce(f32[80,6]{0,1:T(8,128)S(1)} %get-tuple-element.501, f32[80]{0:T(128)S(1)} %get-tuple-element.502, ...), channel_id=1, replica_groups=mesh['pb_0'=4,'pb_1'=4,'pb_2'=2,'pb_3'=2,'ga'=4] {'ga'}, use_global_device_ids=true, to_apply=%region_9.10 | all-reduce | flops 5744 | bytes 45952 | tf_op jit(solution)/shard_map/psum | solution.py:31
  (373 shorter events, 218.3 us)
Async XLA Ops:
  7.2 94.4 %all-gather.2.cloned.1.call-start = ((), (), s32[]{:S(2)}) async-start(), calls=%async_computation.1 | async-start | bytes 2129920 | tf_op jit(solution)/shard_map/all_gather | solution.py:40
  101.6 2.3 copy-start
  101.6 2.3 copy-start.1
  101.6 2.3 copy-start.2
  101.6 2.3 copy-start.3
  474.4 92.4 %all-to-all-start = ((bf16[64,64,256]{2,1,0:T(8,128)(2,1)}), bf16[64,64,256]{2,1,0:T(8,128)(2,1)S(1)}, u32[]{:S(2)}, u32[]{:S(2)}) async-start(bf16[64,64,256]{2,1,0:T(8,128)(2,1)} %copy.31), calls=%async_computation | async-start | bytes 4194304 | tf_op jit(solution)/shard_map/all_to_all | solution.py:26
Sparse Core Ops, SparseCore 0:
  11.3 90.1 all-gather.1
where the time goes:
time: 582 us; the launch traced here: 575 us
  local copies, waits for them, and re-layouts  159 us (27%)
  matrix products  111 us (19%)
  waiting for transfers between devices  89.2 us (15%)
  blocking collectives  84.9 us (15%)
  loops' own time  63.4 us (11%)
  other arithmetic  47.1 us (8%)
  between operations  14.1 us (2%)
    all_gather x1, waiting for transfers between devices, shards(): slab_feats = lax.all_gather(latent, PB, axis=2, tiled=True)[0]  88.5 us
    psum x5, blocking collectives, by_axis(): return functools.reduce(lax.psum, axes, value)  84.9 us
    gather x96, local copies, waits for them, and re-layouts  70.8 us
    another operation x1, loops' own time, shards(): lax.scan(advance, (start_grid, start_totals), inputs_all)  62.7 us
    dynamic_update_slice x32, local copies, waits for them, and re-layouts, advance(): lax.dynamic_update_slice_in_dim(partial_grad, current + results[0][number...  59.4 us
    dot_general x8, matrix products, tile_work(): jnp.dot(w_in, features_in, precision=lax.Precision.HIGHEST, preferred_ele...  42.8 us
    add x32, other arithmetic, advance(): current + results[0][number]  32.5 us
    dot_general x8, matrix products, tile_work(): lax.dot_general(w_out, grad_kernel, (((0,), (0,)), ((), ())), preferred_e...  20.5 us
  transfers between devices with their start and end apart: 2, of which 1 were waited for; matrix products, arithmetic and copies ran while one was open for 1% of the time, Pallas kernels for 0%

commit v1 on v0

v1 whole, which is shorter than its diff:
```python
import functools
import itertools
import math

import jax
import jax.numpy as jnp
from jax import lax
from jax.experimental import pallas as pl
from jax.experimental.pallas import tpu as pltpu
from jax.sharding import Mesh
from jax.sharding import PartitionSpec as P

KN = 8
TILE = 128
WIN = 512
GX = 64
ZS = 4
SPAN = WIN + TILE
BLOCK = 256
PB = ("pb_0", "pb_1", "pb_2", "pb_3")
PB_GA = ("pb_0", "pb_1", "pb_2", "pb_3", "ga")
F32 = jnp.float32
BF16 = jnp.bfloat16
I32 = jnp.int32
NT = (((1,), (1,)), ((), ()))
NN = (((1,), (0,)), ((), ()))


def dot(a, b, dims=NN):
    return lax.dot_general(a, b, dims, preferred_element_type=F32)


def split3(value):
    hi = value.astype(BF16)
    rest = value - hi.astype(F32)
    mid = rest.astype(BF16)
    low = (rest - mid.astype(F32)).astype(BF16)
    return hi, mid, low


def iota(shape, dim):
    return lax.broadcasted_iota(I32, shape, dim)


def unit(shape, row_to_col):
    return jnp.where(row_to_col(iota(shape, 0), iota(shape, 1)), 1.0, 0.0).astype(BF16)


def first_cell(start, cells):
    return jnp.minimum(start // TILE * TILE, cells - SPAN)


def weight_prologue(w_in_ref, b_in_ref, w_out_ref, b_out_ref, a_ref, wo_ref, wt_ref):
    hid = w_in_ref.shape[0]
    ch = w_out_ref.shape[0]
    parts = split3(w_in_ref[...])
    bias = split3(b_in_ref[...])
    total = jnp.zeros((hid, 48), F32)
    for n in range(3):
        place = unit(
            (6, 48),
            lambda r, c, n=n: (c // 16 == n)
            & (((r < 3) & (c % 16 < 9) & (c % 16 % 3 == r)) | ((r >= 3) & (c % 16 == r + 6))),
        )
        total += dot(parts[n], place)
        diag = jnp.where(
            iota((hid, hid), 0) == iota((hid, hid), 1), jnp.broadcast_to(bias[n].astype(F32), (hid, hid)), 0.0
        ).astype(BF16)
        total += dot(diag, unit((hid, 48), lambda r, c, n=n: c == 16 * n + 12))
    a_ref[...] = total.astype(BF16)
    bias = split3(b_out_ref[...])
    total = dot(w_out_ref[...], unit((hid, hid + 16), lambda r, c: r == c))
    for n in range(3):
        diag = jnp.where(
            iota((ch, ch), 0) == iota((ch, ch), 1), jnp.broadcast_to(bias[n].astype(F32), (ch, ch)), 0.0
        ).astype(BF16)
        total += dot(diag, unit((ch, hid + 16), lambda r, c, n=n: c == hid + n))
    wo_ref[...] = total.astype(BF16)
    wt_ref[...] = dot(unit((hid, hid), lambda r, c: r == c), w_out_ref[...], NT).astype(BF16)


def compact(slab_here, slab_ref, rel_ref, info_ref, count_ref):
    tiles = slab_ref.shape[1] // TILE
    group = 8
    rows = group * KN
    upper = unit((TILE, TILE), lambda r, c: r < c)
    ones = jnp.ones((TILE, TILE), BF16)
    earlier = unit((rows, rows), lambda r, c: (r // KN == c // KN) & (c < r))
    same = unit((rows, rows), lambda r, c: r // KN == c // KN)
    lane = iota((rows, TILE), 1)
    counts = []
    for g in range(tiles // group):
        cut = [slice((g * group + n) * TILE, (g * group + n + 1) * TILE) for n in range(group)]
        slabs = jnp.concatenate([slab_ref[:, c] for c in cut], 0)
        rels = jnp.concatenate([rel_ref[:, c] for c in cut], 0)
        live = slabs == slab_here
        live_b = jnp.where(live, 1.0, 0.0).astype(BF16)
        before = dot(live_b, upper).astype(I32)
        row_count = dot(live_b, ones)
        row_start = dot(earlier, row_count.astype(BF16)).astype(I32)
        counts.append(dot(same, row_count.astype(BF16)))
        row_count = row_count.astype(I32)
        item = jnp.where(live, (1 + rels + 1024 * lane) * 128 + (lane - before), 0)
        for bit in range(7):
            step = 1 << bit
            moved = pltpu.roll(item, TILE - step, 1)
            arrives = (moved & step) != 0
            leaves = (item & step) != 0
            item = jnp.where(arrives, moved, jnp.where(leaves, 0, item))
        value = item // 128
        for bit in range(7):
            step = 1 << bit
            value = jnp.where((row_start & step) != 0, pltpu.roll(value, step, 1), value)
        turn = row_start & (TILE - 1)
        number = (lane - turn) & (TILE - 1)
        place = number + row_start
        value = jnp.where(number < row_count, value, 0).astype(F32)
        chunk = place // TILE
        for n in range(group):
            part = slice(n * KN, (n + 1) * KN)
            dense = [
                jnp.sum(jnp.where(chunk[part] == c, value[part], 0.0), axis=0, keepdims=True)
                for c in range(KN)
            ]
            info_ref[g * group + n] = jnp.concatenate(dense, 0)
    for g in range(tiles // group):
        count_ref[g * rows : (g + 1) * rows] = counts[g].astype(I32)


def entry_rows(info, base, slab_here):
    packed = info.astype(I32) - 1
    valid = info > 0.0
    query = jnp.where(valid, packed >> 10, -1)
    rel = jnp.where(valid, packed & 1023, -1)
    cell = base + rel
    return query, rel, cell


def one_hot(index, rows):
    pieces = []
    for first in range(0, rows, TILE):
        near = index - first
        near = jnp.where((near >= 0) & (near < TILE), near, -1).astype(F32).astype(BF16)
        ids = iota((TILE, index.shape[1]), 0).astype(F32).astype(BF16)
        pieces.append(jnp.where(ids == jnp.broadcast_to(near, ids.shape), jnp.ones((), BF16), jnp.zeros((), BF16)))
    return jnp.concatenate(pieces, 0)


def block_forward(info, shift, base, slab_here, query_cols, a_ref, wo_ref):
    hid = a_ref.shape[0]
    query, rel, cell = entry_rows(info, base, slab_here)
    rel = jnp.where(rel >= 0, rel + shift, -1)
    cell = cell + shift
    ch = wo_ref.shape[0]
    here = dot(query_cols, one_hot(query, TILE))
    cot = here[:ch]
    point = here[ch : ch + 16]
    along_x = ((cell >> 8).astype(F32) + 0.5) / GX
    along_y = (((cell >> 2) & (GX - 1)).astype(F32) + 0.5) / GX
    along_z = ((cell & (ZS - 1)).astype(F32) + (slab_here * ZS).astype(F32) + 0.5) / GX
    row = iota((16, info.shape[1]), 0)
    features = jnp.where(
        row < 9,
        point,
        jnp.where(
            row == 9,
            along_x,
            jnp.where(row == 10, along_y, jnp.where(row == 11, along_z, jnp.where(row == 12, 1.0, 0.0))),
        ),
    ).astype(BF16)
    preact = dot(a_ref[...], jnp.concatenate([features] * 3, 0))
    cdf = 0.5 * (1.0 + lax.erf(preact * math.sqrt(0.5)))
    slope = cdf + preact * jnp.exp(preact * preact * -0.5) * (1.0 / math.sqrt(2.0 * math.pi))
    hidden = (preact * cdf).astype(BF16)
    extra = jnp.where(iota((16, info.shape[1]), 0) < 3, 1.0, 0.0).astype(BF16)
    hidden = jnp.concatenate([hidden, extra], 0)
    kernel = dot(wo_ref[...], hidden)
    grad_cell = (kernel * cot).astype(BF16)
    return rel, cot, features, slope, hidden, grad_cell


def compute_kernel(
    offsets_ref, points_ref, cot_ref, slab_ref, rel_ref, feats_ref,
    w_in_ref, b_in_ref, w_out_ref, b_out_ref,
    partial_ref, totals_ref,
    acc_ref, info_ref, count_ref, count_smem, a_ref, wo_ref, wt_ref, sem,
):
    slab_here = lax.axis_index("ga")
    cells = acc_ref.shape[1]
    ch = cot_ref.shape[0]
    hid = w_in_ref.shape[0]
    tiles = slab_ref.shape[1] // TILE
    weight_prologue(w_in_ref, b_in_ref, w_out_ref, b_out_ref, a_ref, wo_ref, wt_ref)
    compact(slab_here, slab_ref, rel_ref, info_ref, count_ref)
    copy = pltpu.make_async_copy(count_ref, count_smem, sem)
    copy.start()
    acc_ref[...] = jnp.zeros_like(acc_ref)
    totals_ref[...] = jnp.zeros_like(totals_ref)
    copy.wait()

    def tile_step(t, carry):
        lanes = pl.ds(pl.multiple_of(t * TILE, TILE), TILE)
        start = offsets_ref[0, t]
        base = pl.multiple_of(first_cell(start, cells), TILE)
        shift = start - base
        q_hi, q_mid, q_low = split3(points_ref[:, lanes])
        parts = jnp.concatenate(
            [q_hi.astype(F32), q_mid.astype(F32), q_low.astype(F32), jnp.zeros((7, TILE), F32)], 0
        ).astype(BF16)
        query_cols = jnp.concatenate([cot_ref[:, lanes], parts], 0)
        window = pl.ds(base, SPAN)
        blocks = (count_smem[t * KN, 0] + (BLOCK - 1)) // BLOCK

        def block_step(n, carry):
            info = jnp.concatenate(
                [info_ref[t, pl.ds(2 * n, 1), :], info_ref[t, pl.ds(2 * n + 1, 1), :]], 1
            )
            rel, cot, features, slope, hidden, grad_cell = block_forward(
                info, shift, base, slab_here, query_cols, a_ref, wo_ref
            )
            spread = one_hot(rel, SPAN)
            acc_ref[:, window] += dot(grad_cell, spread, NT)
            feats = dot(feats_ref[:, window], spread)
            grad_kernel = (feats * cot).astype(BF16)
            totals_ref[0:ch, 0 : hid + 16] += dot(grad_kernel, hidden, NT)
            grad_pre = dot(wt_ref[...], grad_kernel) * slope
            hi = grad_pre.astype(BF16)
            low = (grad_pre - hi.astype(F32)).astype(BF16)
            totals_ref[ch : ch + 16, 0:hid] += dot(features, hi, NT) + dot(features, low, NT)
            return carry

        return lax.fori_loop(0, blocks, block_step, carry)

    lax.fori_loop(0, tiles, tile_step, 0)
    wide = partial_ref.shape[-1]
    for p, (x, y, h, c) in enumerate(itertools.product(range(4), range(4), range(2), range(2))):
        first, second = ((x, y), (y, x))[c]
        partial_ref[c, first, second, h] = acc_ref[:, p * wide : (p + 1) * wide].astype(BF16)


def local_work(offsets, points, cot, slabs, rels, feats, w_in, b_in, w_out, b_out):
    ch, hid = w_out.shape
    cells = feats.shape[1]
    tiles = slabs.shape[1] // TILE
    vmem = pl.BlockSpec(memory_space=pltpu.VMEM)
    smem = pl.BlockSpec(memory_space=pltpu.SMEM)
    return pl.pallas_call(
        compute_kernel,
        out_shape=(
            jax.ShapeDtypeStruct((2, 4, 4, 2, ch, cells // 64), BF16),
            jax.ShapeDtypeStruct((ch + 16, TILE), F32),
        ),
        in_specs=[smem] + [vmem] * 9,
        out_specs=(vmem, vmem),
        scratch_shapes=[
            pltpu.VMEM((ch, cells), F32),
            pltpu.VMEM((tiles, KN, TILE), F32),
            pltpu.VMEM((tiles * KN, TILE), I32),
            pltpu.SMEM((tiles * KN, TILE), I32),
            pltpu.VMEM((hid, 48), BF16),
            pltpu.VMEM((ch, hid + 16), BF16),
            pltpu.VMEM((hid, ch), BF16),
            pltpu.SemaphoreType.DMA,
        ],
        compiler_params=pltpu.CompilerParams(vmem_limit_bytes=40 << 20),
        cost_estimate=pl.CostEstimate(flops=10**9, bytes_accessed=10**7, transcendentals=0),
        name="local_work",
    )(offsets, points, cot, slabs, rels, feats, w_in, b_in, w_out, b_out)


MESH_ID = pl.DeviceIdType.MESH


class Place:
    def __init__(self):
        self.x, self.y, self.h, self.c = (lax.axis_index(name) for name in PB)
        self.g = lax.axis_index("ga")
        self.first = self.x * (1 - self.c) + self.y * self.c
        self.second = self.y * (1 - self.c) + self.x * self.c

    def at(self, first=None, second=None, h=None, c=None, g=None):
        first = self.first if first is None else first
        second = self.second if second is None else second
        core = self.c
        return (
            first * (1 - core) + second * core,
            second * (1 - core) + first * core,
            self.h if h is None else h,
            core if c is None else c,
            self.g if g is None else g,
        )

    def sibling(self):
        return (self.x, self.y, self.h, 1 - self.c, self.g)


def greet(devices):
    barrier = pltpu.get_barrier_semaphore()
    for device in devices:
        pl.semaphore_signal(barrier, inc=1, device_id=device, device_id_type=MESH_ID)
    pl.semaphore_wait(barrier, len(devices))


def gather_kernel(block_ref, out_ref, send_sem, recv_sem):
    me = Place()
    wide = block_ref.shape[1]
    sends = []

    def number(first, second, h, c):
        x = first * (1 - me.c) + second * me.c
        y = second * (1 - me.c) + first * me.c
        return ((x * 4 + y) * 2 + h) * 2 + c

    def spot(p):
        return out_ref.at[:, pl.ds(pl.multiple_of(p * wide, wide), wide)]

    def send(source, p, device):
        copy = pltpu.make_async_remote_copy(
            src_ref=source,
            dst_ref=spot(p),
            send_sem=send_sem.at[len(sends)],
            recv_sem=recv_sem.at[p],
            device_id=device,
            device_id_type=MESH_ID,
        )
        copy.start()
        sends.append(copy)

    def arrived(p):
        pltpu.make_async_remote_copy(
            src_ref=spot(p),
            dst_ref=spot(p),
            send_sem=send_sem.at[0],
            recv_sem=recv_sem.at[p],
            device_id=me.sibling(),
            device_id_type=MESH_ID,
        ).wait_recv()

    steps = (1, 3, 2)
    near = [me.at(first=(me.first + n) % 4) for n in steps]
    far = [me.at(second=(me.second + n) % 4) for n in steps]
    across = me.at(h=1 - me.h)
    greet([me.sibling(), across] + near + far)
    mine = number(me.first, me.second, me.h, me.c)
    for device in [across] + near + far + [me.sibling()]:
        send(block_ref, mine, device)
    out_ref[:, pl.ds(pl.multiple_of(mine * wide, wide), wide)] = block_ref[...]

    def pass_on(p, devices):
        arrived(p)
        for device in devices + [me.sibling()]:
            send(spot(p), p, device)

    other = 1 - me.h
    for n in steps:
        pass_on(number((me.first + n) % 4, me.second, me.h, me.c), far)
    pass_on(number(me.first, me.second, other, me.c), near + far)
    for n in steps:
        for m in (0, 1, 3, 2):
            pass_on(number((me.first + m) % 4, (me.second + n) % 4, me.h, me.c), [])
    for n in steps:
        pass_on(number((me.first + n) % 4, me.second, other, me.c), far)
    for n in steps:
        for m in (0, 1, 3, 2):
            pass_on(number((me.first + m) % 4, (me.second + n) % 4, other, me.c), [])
    for x in range(4):
        for y in range(4):
            for h in range(2):
                arrived(((x * 4 + y) * 2 + h) * 2 + 1 - me.c)
    for copy in sends:
        copy.wait_send()


def gather_slab(block, owners):
    ch, wide = block.shape
    vmem = pl.BlockSpec(memory_space=pltpu.VMEM)
    return pl.pallas_call(
        gather_kernel,
        out_shape=jax.ShapeDtypeStruct((ch, wide * owners), BF16),
        in_specs=[vmem],
        out_specs=vmem,
        scratch_shapes=[pltpu.SemaphoreType.DMA((63,)), pltpu.SemaphoreType.DMA((64,))],
        compiler_params=pltpu.CompilerParams(
            collective_id=0, has_side_effects=True, vmem_limit_bytes=16 << 20
        ),
        name="gather_slab",
    )(block)


def reduce_kernel(
    partial_ref, totals_ref, out_ref, sums_ref,
    r0_ref, s0_ref, r1_ref, s1_ref, r2_ref, s2_ref, r3_ref,
    ta_ref, tf_ref, ts_ref, tz_ref, th_ref,
    sem0, sem1, sem2, sem3, tsem_a, tsem_f, tsem_s, tsem_z, tsem_h,
):
    me = Place()
    half = ta_ref.shape[0]
    sends = []

    def send(source, target, sems, device, recv_index, send_index):
        copy = pltpu.make_async_remote_copy(
            src_ref=source,
            dst_ref=target,
            send_sem=sems.at[(0,) + send_index],
            recv_sem=sems.at[(1,) + recv_index],
            device_id=device,
            device_id_type=MESH_ID,
        )
        copy.start()
        sends.append(copy)

    def arrived(target, sems, recv_index):
        pltpu.make_async_remote_copy(
            src_ref=target,
            dst_ref=target,
            send_sem=sems.at[(0,) + recv_index],
            recv_sem=sems.at[(1,) + recv_index],
            device_id=me.sibling(),
            device_id_type=MESH_ID,
        ).wait_recv()

    steps = (2, 1, 3)
    firsts = [(me.first + n) % 4 for n in steps]
    seconds = [(me.second + n) % 4 for n in steps]
    depth = me.h * 4 + me.g
    depths = [(depth + n) % 8 for n in range(1, 8)]
    line = [me.at(h=d // 4, g=d % 4) for d in depths]
    across = me.at(h=1 - me.h)
    greet(
        [me.sibling()]
        + [me.at(first=f) for f in firsts]
        + [me.at(second=s) for s in seconds]
        + line
    )

    own_half = pl.ds(pl.multiple_of(me.c * half, 8), half)
    other_half = pl.ds(pl.multiple_of((1 - me.c) * half, 8), half)
    send(totals_ref.at[other_half], ta_ref, tsem_a, me.sibling(), (0,), (0,))
    for n in steps + (0,):
        f = (me.second + n) % 4
        send(partial_ref.at[1 - me.c, f], r0_ref.at[f], sem0, me.sibling(), (f,), (f,))
    for n, f in zip(steps, firsts):
        arrived(r0_ref.at[f], sem0, (f,))
        s0_ref[n - 1] = (partial_ref[me.c, f].astype(F32) + r0_ref[f].astype(F32)).astype(BF16)
        for m in steps + (0,):
            s = (me.second + m) % 4
            send(s0_ref.at[n - 1, s], r1_ref.at[3 - n, s], sem1, me.at(first=f), (3 - n, s), (n - 1, s))

    arrived(ta_ref, tsem_a, (0,))
    tf_ref[me.first] = totals_ref[own_half] + ta_ref[...]
    for n, f in zip(steps, firsts):
        send(tf_ref.at[me.first], tf_ref.at[me.first], tsem_f, me.at(first=f), (me.first,), (n,))

    arrived(r0_ref.at[me.first], sem0, (me.first,))

    def collect(s):
        total = partial_ref[me.c, me.first, s].astype(F32) + r0_ref[me.first, s].astype(F32)
        for n in range(3):
            arrived(r1_ref.at[n, s], sem1, (n, s))
            total += r1_ref[n, s].astype(F32)
        return total

    for n, s in zip(steps, seconds):
        s1_ref[n - 1] = collect(s).astype(BF16)
        send(s1_ref.at[n - 1], r2_ref.at[3 - n], sem2, me.at(second=s), (3 - n,), (n - 1,))
        if n == steps[0]:
            for f in firsts:
                arrived(tf_ref.at[f], tsem_f, (f,))
            ts_ref[me.second] = tf_ref[0] + tf_ref[1] + tf_ref[2] + tf_ref[3]
            for k, t in zip(steps, seconds):
                send(ts_ref.at[me.second], ts_ref.at[me.second], tsem_s, me.at(second=t), (me.second,), (k,))
    total = collect(me.second)
    for s in seconds:
        arrived(ts_ref.at[s], tsem_s, (s,))
    tz_ref[depth] = ts_ref[0] + ts_ref[1] + ts_ref[2] + ts_ref[3]
    for n, device in enumerate(line):
        send(tz_ref.at[depth], tz_ref.at[depth], tsem_z, device, (depth,), (n,))
    for n in range(3):
        arrived(r2_ref.at[n], sem2, (n,))
        total += r2_ref[n].astype(F32)
    s2_ref[...] = total
    s1_ref[3, 0] = s2_ref[1 - me.h].astype(BF16)
    send(s1_ref.at[3, 0], r3_ref, sem3, across, (0,), (0,))
    for d in depths:
        arrived(tz_ref.at[d], tsem_z, (d,))
    total = tz_ref[0]
    for d in range(1, 8):
        total += tz_ref[d]
    th_ref[me.c] = total
    send(th_ref.at[me.c], th_ref.at[me.c], tsem_h, me.sibling(), (me.c,), (0,))
    arrived(r3_ref, sem3, (0,))
    out_ref[...] = s2_ref[me.h] + r3_ref[...].astype(F32)
    arrived(th_ref.at[1 - me.c], tsem_h, (1 - me.c,))
    sums_ref[0:half] = th_ref[0]
    sums_ref[half : 2 * half] = th_ref[1]
    for copy in sends:
        copy.wait_send()


def reduce_all(partial, totals):
    ch, wide = partial.shape[-2:]
    rows, lanes = totals.shape
    half = rows // 2
    vmem = pl.BlockSpec(memory_space=pltpu.VMEM)
    dma = pltpu.SemaphoreType.DMA
    return pl.pallas_call(
        reduce_kernel,
        out_shape=(
            jax.ShapeDtypeStruct((ch, wide), F32),
            jax.ShapeDtypeStruct((rows, lanes), F32),
        ),
        in_specs=[vmem, vmem],
        out_specs=(vmem, vmem),
        scratch_shapes=[
            pltpu.VMEM((4, 4, 2, ch, wide), BF16),
            pltpu.VMEM((3, 4, 2, ch, wide), BF16),
            pltpu.VMEM((3, 4, 2, ch, wide), BF16),
            pltpu.VMEM((4, 2, ch, wide), BF16),
            pltpu.VMEM((3, 2, ch, wide), BF16),
            pltpu.VMEM((2, ch, wide), F32),
            pltpu.VMEM((ch, wide), BF16),
            pltpu.VMEM((half, lanes), F32),
            pltpu.VMEM((4, half, lanes), F32),
            pltpu.VMEM((4, half, lanes), F32),
            pltpu.VMEM((8, half, lanes), F32),
            pltpu.VMEM((2, half, lanes), F32),
            dma((2, 4)),
            dma((2, 3, 4)),
            dma((2, 3)),
            dma((2, 1)),
            dma((2, 1)),
            dma((2, 4)),
            dma((2, 4)),
            dma((2, 8)),
            dma((2, 2)),
        ],
        compiler_params=pltpu.CompilerParams(
            collective_id=1, has_side_effects=True, vmem_limit_bytes=24 << 20
        ),
        name="reduce_all",
    )(partial, totals)


def shards(query_points, cotangent, slab_ids, rel_cells, offsets, latent, w_in, b_in, w_out, b_out):
    ch, hid = w_out.shape
    slab_feats = gather_slab(latent[0], lax.axis_size(PB))
    partial, totals = local_work(
        offsets, query_points, cotangent, slab_ids, rel_cells, slab_feats, w_in, b_in[None], w_out, b_out[None]
    )
    owned, totals = reduce_all(partial, totals)
    scale = float(query_points.shape[1] * lax.axis_size(PB)) ** (-0.5)
    totals = totals * scale
    w_out_grad = totals[:ch, :hid]
    b_out_grad = totals[:ch, hid]
    rows = totals[ch:, :hid]
    w_in_grad = jnp.concatenate([rows[0:3] + rows[3:6] + rows[6:9], rows[9:12]], 0).T
    b_in_grad = rows[12]
    return owned[None], w_in_grad, b_in_grad, w_out_grad, b_out_grad


def solution(mesh):
    finer = Mesh(
        mesh.devices.reshape(4, 4, 2, 2, mesh.shape["ga"]), ("pb_0", "pb_1", "pb_2", "pb_3", "ga")
    )
    in_specs = (
        P(None, PB),
        P(None, PB),
        P(None, PB),
        P(None, PB),
        P("ga", PB),
        P("ga", None, PB),
        P(),
        P(),
        P(),
        P(),
    )
    out_specs = (P("ga", None, PB), P(), P(), P(), P())
    return jax.shard_map(
        shards, mesh=finer, in_specs=in_specs, out_specs=out_specs, check_vma=False
    )
```

time: 582 us -> 93.7 us (0.16); the launches traced: 575 us -> 93.5 us
  local copies, waits for them, and re-layouts: 159 us -> 4.04 us
  matrix products: 111 us -> 0 us
  waiting for transfers between devices: 89.2 us -> 0 us
  Pallas kernels: 0 us -> 88 us
  blocking collectives: 84.9 us -> 0 us
  loops' own time: 63.4 us -> 0 us
  other arithmetic: 47.1 us -> 0.61 us
  between operations: 14.1 us -> 0.77 us
    dot_general x48 -> x0, matrix products: 111 us -> none  [the longest x8 42.8 us: tile_work(): jnp.dot(w_in, features_in, precision=lax.Precision.HIGHEST, preferred_ele...]
    all_gather x1 -> x0, waiting for transfers between devices: 88.5 us -> none  [shards(): slab_feats = lax.all_gather(latent, PB, axis=2, tiled=True)[0]]
    pallas_call x0 -> x3, Pallas kernels: none -> 88 us  [the longest x1 35.5 us: local_work(): pl.pallas_call(compute_kernel, out_shape=(jax.ShapeDtypeStruct((2, 4, 4,...]
    psum x5 -> x0, blocking collectives: 84.9 us -> none  [by_axis(): return functools.reduce(lax.psum, axes, value)]
    gather x96 -> x0, local copies, waits for them, and re-layouts: 70.8 us -> none
    another operation x9 -> x0, loops' own time: 63.4 us -> none  [the longest x1 62.7 us: shards(): lax.scan(advance, (start_grid, start_totals), inputs_all)]
    dynamic_update_slice x32 -> x0, local copies, waits for them, and re-layouts: 59.4 us -> none  [advance(): lax.dynamic_update_slice_in_dim(partial_grad, current + results[0][number...]
    add x48 -> x1, other arithmetic: 32.7 us -> 0.01 us  [shards(): rows[0:3] + rows[3:6] + rows[6:9]]
  transfers between devices with their start and end apart: 2 -> 0, of which waited for: 1 -> 0; matrix products, arithmetic and copies ran while one was open for 1% -> 0% of each run, Pallas kernels for 0% -> 0%
where the time goes in v1:
time: 93.7 us; the launch traced here: 93.5 us
  Pallas kernels  88 us (94%)
  local copies, waits for them, and re-layouts  4.04 us (4%)
    pallas_call x1, Pallas kernels, local_work(): pl.pallas_call(compute_kernel, out_shape=(jax.ShapeDtypeStruct((2, 4, 4,...  35.5 us
    pallas_call x1, Pallas kernels, gather_slab(): pl.pallas_call(gather_kernel, out_shape=jax.ShapeDtypeStruct((ch, wide *...  26.8 us
    pallas_call x1, Pallas kernels, reduce_all(): pl.pallas_call(reduce_kernel, out_shape=(jax.ShapeDtypeStruct((ch, wide),...  25.7 us
    unnamed x20, local copies, waits for them, and re-layouts  2.22 us

profile of v1, /device:TPU:1, one launch (start us, length us, event | category | flops | bytes accessed | tf_op | source)
XLA Modules:
  0.0 93.5 jit_solution(10166824434932877365)
XLA Ops:
  0.6 0.0 copy-start.8
  0.6 0.0 copy-start.5
  0.7 0.0 copy-start.7
  0.7 0.0 copy-start.6
  0.7 0.8 copy.16.w_in_ref
  1.5 0.0 copy-start
  1.5 0.8 copy-done
  2.2 0.0 copy-start.1
  2.2 0.0 copy-start.2
  2.2 0.0 copy-start.3
  2.2 0.0 copy-start.4
  2.2 26.8 %gather_slab.1.feats_ref = bf16[64,16384]{1,0:T(8,128)(2,1)S(1)} custom-call(bf16[64,256]{1,0:T(8,128)(2,1)S(1)} %bitcast.9), custom_call_target="tpu_custom_call" | custom-call | tf_op jit(solution)/shard_map/gather_slab/pallas_call | solution.py:377
  29.1 0.0 copy-done.8
  29.1 0.0 copy-done.5
  29.1 0.0 copy-done.7
  29.1 0.0 copy-done.6
  29.1 0.0 copy-done.1
  29.1 0.0 copy-done.2
  29.2 0.0 copy-done.3
  29.2 0.0 copy-done.4
  29.2 35.5 %local_work.1 = (bf16[2,4,4,2,64,256]{5,4,3,2,1,0:T(8,128)(2,1)S(1)}, f32[80,128]{1,0:T(8,128)S(1)}) custom-call(s32[1,32]{1,0:T(1,128)S(1)} %copy-done.6, f32[3,4096]{1,0:T(4,128)S(1)} %copy-done.4, bf16[64,4096]{1,0:T(8,128)(2,1)S(1)} %copy-done.1, s32[8,4096]{1,0:T(8,128)S(1)} %copy-done.2, s32[8,4096]{1,0:T(8,128)S(1)} %copy-done.3, ...), custom_call_target="tpu_custom_call" | custom-call | flops 1000000000 | bytes 10000000 | tf_op jit(solution)/shard_map/local_work/pallas_call | solution.py:247
  64.7 25.7 %reduce_all.1 = (f32[64,256]{1,0:T(8,128)S(1)}, f32[80,128]{1,0:T(8,128)S(1)}) custom-call(bf16[2,4,4,2,64,256]{5,4,3,2,1,0:T(8,128)(2,1)S(1)} %get-tuple-element.9.partial_ref, f32[80,128]{1,0:T(8,128)S(1)} %get-tuple-element.10.totals_ref), custom_call_target="tpu_custom_call" | custom-call | tf_op jit(solution)/shard_map/reduce_all/pallas_call | solution.py:506
  90.4 0.5 slice_bitcast_fusion
  90.9 0.7 slice_reduce_fusion
  91.6 0.6 slice.39
  92.2 0.6 maximum_bitcast_fusion
  92.8 0.6 copy.18
  (2 shorter events, 0.0 us)
Async XLA Ops:
  0.6 28.5 %copy-start.8 = (f32[64]{0:T(128)S(1)}, f32[64]{0:T(128)}, u32[]{:S(2)}) copy-start(f32[64]{0:T(128)} %param.19) | copy-start | bytes 772
  0.6 28.5 %copy-start.5 = (bf16[64,80]{1,0:T(8,128)(2,1)S(1)}, bf16[64,80]{1,0:T(8,128)(2,1)}, u32[]{:S(2)}) copy-start(bf16[64,80]{1,0:T(8,128)(2,1)} %w_out_ref.1) | copy-start | bytes 30724
  0.7 28.5 %copy-start.7 = (f32[80]{0:T(128)S(1)}, f32[80]{0:T(128)}, u32[]{:S(2)}) copy-start(f32[80]{0:T(128)} %param.17) | copy-start | bytes 964
  0.7 28.5 %copy-start.6 = (s32[1,32]{1,0:T(1,128)S(1)}, s32[1,32]{1,0:T(1,128)}, u32[]{:S(2)}) copy-start(s32[1,32]{1,0:T(1,128)} %offsets_ref.1) | copy-start | bytes 388
  1.5 0.8 copy-start
  2.2 26.9 %copy-start.1 = (bf16[64,4096]{1,0:T(8,128)(2,1)S(1)}, bf16[64,4096]{1,0:T(8,128)(2,1)}, u32[]{:S(2)}) copy-start(bf16[64,4096]{1,0:T(8,128)(2,1)} %cot_ref.1) | copy-start | bytes 1572868
  2.2 26.9 %copy-start.2 = (s32[8,4096]{1,0:T(8,128)S(1)}, s32[8,4096]{1,0:T(8,128)}, u32[]{:S(2)}) copy-start(s32[8,4096]{1,0:T(8,128)} %slab_ref.1) | copy-start | bytes 393220
  2.2 26.9 %copy-start.3 = (s32[8,4096]{1,0:T(8,128)S(1)}, s32[8,4096]{1,0:T(8,128)}, u32[]{:S(2)}) copy-start(s32[8,4096]{1,0:T(8,128)} %rel_ref.1) | copy-start | bytes 393220
  2.2 26.9 %copy-start.4 = (f32[3,4096]{1,0:T(4,128)S(1)}, f32[3,4096]{1,0:T(4,128)}, u32[]{:S(2)}) copy-start(f32[3,4096]{1,0:T(4,128)} %points_ref.1) | copy-start | bytes 147460

commit v2 on v1

--- a/solution.py
+++ b/solution.py
@@ -17,6 +17,7 @@
 ZS = 4
 SPAN = WIN + TILE
 BLOCK = 256
+GROUP = 4
 PB = ("pb_0", "pb_1", "pb_2", "pb_3")
 PB_GA = ("pb_0", "pb_1", "pb_2", "pb_3", "ga")
 F32 = jnp.float32
@@ -81,191 +82,119 @@
 
 def compact(slab_here, slab_ref, rel_ref, info_ref, count_ref):
     tiles = slab_ref.shape[1] // TILE
-    group = 8
-    rows = group * KN
+    rows = tiles * KN
     upper = unit((TILE, TILE), lambda r, c: r < c)
     ones = jnp.ones((TILE, TILE), BF16)
     earlier = unit((rows, rows), lambda r, c: (r // KN == c // KN) & (c < r))
-    same = unit((rows, rows), lambda r, c: r // KN == c // KN)
     lane = iota((rows, TILE), 1)
-    counts = []
-    for g in range(tiles // group):
-        cut = [slice((g * group + n) * TILE, (g * group + n + 1) * TILE) for n in range(group)]
-        slabs = jnp.concatenate([slab_ref[:, c] for c in cut], 0)
-        rels = jnp.concatenate([rel_ref[:, c] for c in cut], 0)
-        live = slabs == slab_here
-        live_b = jnp.where(live, 1.0, 0.0).astype(BF16)
-        before = dot(live_b, upper).astype(I32)
-        row_count = dot(live_b, ones)
-        row_start = dot(earlier, row_count.astype(BF16)).astype(I32)
-        counts.append(dot(same, row_count.astype(BF16)))
-        row_count = row_count.astype(I32)
-        item = jnp.where(live, (1 + rels + 1024 * lane) * 128 + (lane - before), 0)
-        for bit in range(7):
-            step = 1 << bit
-            moved = pltpu.roll(item, TILE - step, 1)
-            arrives = (moved & step) != 0
-            leaves = (item & step) != 0
-            item = jnp.where(arrives, moved, jnp.where(leaves, 0, item))
-        value = item // 128
-        for bit in range(7):
-            step = 1 << bit
-            value = jnp.where((row_start & step) != 0, pltpu.roll(value, step, 1), value)
-        turn = row_start & (TILE - 1)
-        number = (lane - turn) & (TILE - 1)
-        place = number + row_start
-        value = jnp.where(number < row_count, value, 0).astype(F32)
-        chunk = place // TILE
-        for n in range(group):
-            part = slice(n * KN, (n + 1) * KN)
-            dense = [
-                jnp.sum(jnp.where(chunk[part] == c, value[part], 0.0), axis=0, keepdims=True)
-                for c in range(KN)
-            ]
-            info_ref[g * group + n] = jnp.concatenate(dense, 0)
-    for g in range(tiles // group):
-        count_ref[g * rows : (g + 1) * rows] = counts[g].astype(I32)
-
-
-def entry_rows(info, base, slab_here):
-    packed = info.astype(I32) - 1
-    valid = info > 0.0
-    query = jnp.where(valid, packed >> 10, -1)
-    rel = jnp.where(valid, packed & 1023, -1)
-    cell = base + rel
-    return query, rel, cell
+    cut = [slice(n * TILE, (n + 1) * TILE) for n in range(tiles)]
+    live = jnp.concatenate([slab_ref[:, c] for c in cut], 0) == slab_here
+    rels = jnp.concatenate([rel_ref[:, c] for c in cut], 0)
+    live_b = jnp.where(live, 1.0, 0.0).astype(BF16)
+    before = dot(live_b, upper).astype(I32)
+    row_count = dot(live_b, ones)
+    row_start = dot(earlier, row_count.astype(BF16)).astype(I32)
+    count = dot(unit((tiles, rows), lambda r, c: c // KN == r), row_count.astype(BF16))
+    count = jnp.where(iota((tiles, TILE), 0) == iota((tiles, TILE), 1), count, 0.0)
+    count_ref[...] = jnp.broadcast_to(jnp.sum(count, axis=0, keepdims=True), (8, TILE)).astype(I32)
+    row_count = row_count.astype(I32)
+    item = jnp.where(live, (1 + rels + 1024 * lane) * 128 + (lane - before), 0)
+    for bit in range(7):
+        step = 1 << bit
+        moved = pltpu.roll(item, TILE - step, 1)
+        item = jnp.where((moved & step) != 0, moved, jnp.where((item & step) != 0, 0, item))
+    value = item >> 7
+    for bit in range(7):
+        step = 1 << bit
+        value = jnp.where((row_start & step) != 0, pltpu.roll(value, step, 1), value)
+    number = (lane - row_start) & (TILE - 1)
+    chunk = (number + row_start) >> 7
+    value = jnp.where(number < row_count, value, 0).astype(F32)
+    for n in range(tiles):
+        part = slice(n * KN, (n + 1) * KN)
+        dense = [
+            jnp.sum(jnp.where(chunk[part] == c, value[part], 0.0), axis=0, keepdims=True)
+            for c in range(KN)
+        ]
+        info_ref[n] = jnp.concatenate(dense, 0)
 
 
 def one_hot(index, rows):
+    ids = iota((TILE, index.shape[1]), 0).astype(F32).astype(BF16)
     pieces = []
     for first in range(0, rows, TILE):
         near = index - first
-        near = jnp.where((near >= 0) & (near < TILE), near, -1).astype(F32).astype(BF16)
-        ids = iota((TILE, index.shape[1]), 0).astype(F32).astype(BF16)
+        near = jnp.where((near >= 0.0) & (near < TILE), near, -1.0).astype(BF16)
         pieces.append(jnp.where(ids == jnp.broadcast_to(near, ids.shape), jnp.ones((), BF16), jnp.zeros((), BF16)))
     return jnp.concatenate(pieces, 0)
 
 
-def block_forward(info, shift, base, slab_here, query_cols, a_ref, wo_ref):
-    hid = a_ref.shape[0]
-    query, rel, cell = entry_rows(info, base, slab_here)
-    rel = jnp.where(rel >= 0, rel + shift, -1)
-    cell = cell + shift
+def query_columns(points, cot):
+    q_hi, q_mid, q_low = split3(points)
+    parts = jnp.concatenate(
+        [q_hi.astype(F32), q_mid.astype(F32), q_low.astype(F32), jnp.zeros((7, points.shape[1]), F32)], 0
+    ).astype(BF16)
+    return jnp.concatenate([cot, parts], 0)
+
+
+def entries_forward(infos, starts, cells, slab_here, columns, a_ref, wo_ref):
     ch = wo_ref.shape[0]
-    here = dot(query_cols, one_hot(query, TILE))
-    cot = here[:ch]
-    point = here[ch : ch + 16]
-    along_x = ((cell >> 8).astype(F32) + 0.5) / GX
-    along_y = (((cell >> 2) & (GX - 1)).astype(F32) + 0.5) / GX
-    along_z = ((cell & (ZS - 1)).astype(F32) + (slab_here * ZS).astype(F32) + 0.5) / GX
-    row = iota((16, info.shape[1]), 0)
-    features = jnp.where(
-        row < 9,
-        point,
-        jnp.where(
-            row == 9,
-            along_x,
-            jnp.where(row == 10, along_y, jnp.where(row == 11, along_z, jnp.where(row == 12, 1.0, 0.0))),
-        ),
-    ).astype(BF16)
-    preact = dot(a_ref[...], jnp.concatenate([features] * 3, 0))
-    cdf = 0.5 * (1.0 + lax.erf(preact * math.sqrt(0.5)))
-    slope = cdf + preact * jnp.exp(preact * preact * -0.5) * (1.0 / math.sqrt(2.0 * math.pi))
-    hidden = (preact * cdf).astype(BF16)
-    extra = jnp.where(iota((16, info.shape[1]), 0) < 3, 1.0, 0.0).astype(BF16)
-    hidden = jnp.concatenate([hidden, extra], 0)
-    kernel = dot(wo_ref[...], hidden)
-    grad_cell = (kernel * cot).astype(BF16)
-    return rel, cot, features, slope, hidden, grad_cell
-
-
-def compute_kernel(
-    offsets_ref, points_ref, cot_ref, slab_ref, rel_ref, feats_ref,
-    w_in_ref, b_in_ref, w_out_ref, b_out_ref,
-    partial_ref, totals_ref,
-    acc_ref, info_ref, count_ref, count_smem, a_ref, wo_ref, wt_ref, sem,
-):
-    slab_here = lax.axis_index("ga")
-    cells = acc_ref.shape[1]
-    ch = cot_ref.shape[0]
-    hid = w_in_ref.shape[0]
-    tiles = slab_ref.shape[1] // TILE
-    weight_prologue(w_in_ref, b_in_ref, w_out_ref, b_out_ref, a_ref, wo_ref, wt_ref)
-    compact(slab_here, slab_ref, rel_ref, info_ref, count_ref)
-    copy = pltpu.make_async_copy(count_ref, count_smem, sem)
-    copy.start()
-    acc_ref[...] = jnp.zeros_like(acc_ref)
-    totals_ref[...] = jnp.zeros_like(totals_ref)
-    copy.wait()
-
-    def tile_step(t, carry):
-        lanes = pl.ds(pl.multiple_of(t * TILE, TILE), TILE)
-        start = offsets_ref[0, t]
-        base = pl.multiple_of(first_cell(start, cells), TILE)
-        shift = start - base
-        q_hi, q_mid, q_low = split3(points_ref[:, lanes])
-        parts = jnp.concatenate(
-            [q_hi.astype(F32), q_mid.astype(F32), q_low.astype(F32), jnp.zeros((7, TILE), F32)], 0
+    rels, centres, heres = [], [], []
+    for info, start, column in zip(infos, starts, columns):
+        packed = info.astype(I32) - 1
+        valid = info > 0.0
+        query = jnp.where(valid, packed >> 10, -1).astype(F32)
+        own = packed & 1023
+        cell = jnp.where(valid, start + own, 0)
+        rels.append(jnp.where(valid, own + (start - first_cell(start, cells)), -1).astype(F32))
+        centres.append(
+            (
+                ((cell >> 8).astype(F32) + 0.5) / GX,
+                (((cell >> 2) & (GX - 1)).astype(F32) + 0.5) / GX,
+                ((cell & (ZS - 1)).astype(F32) + (slab_here * ZS).astype(F32) + 0.5) / GX,
+            )
+        )
+        heres.append(dot(column, one_hot(query, TILE)))
+    features, preacts = [], []
+    for here, (along_x, along_y, along_z) in zip(heres, centres):
+        row = iota((16, here.shape[1]), 0)
+        feature = jnp.where(
+            row < 9,
+            here[ch : ch + 16],
+            jnp.where(
+                row == 9,
+                along_x,
+                jnp.where(row == 10, along_y, jnp.where(row == 11, along_z, jnp.where(row == 12, 1.0, 0.0))),
+            ),
         ).astype(BF16)
-        query_cols = jnp.concatenate([cot_ref[:, lanes], parts], 0)
-        window = pl.ds(base, SPAN)
-        blocks = (count_smem[t * KN, 0] + (BLOCK - 1)) // BLOCK
-
-        def block_step(n, carry):
-            info = jnp.concatenate(
-                [info_ref[t, pl.ds(2 * n, 1), :], info_ref[t, pl.ds(2 * n + 1, 1), :]], 1
-            )
-            rel, cot, features, slope, hidden, grad_cell = block_forward(
-                info, shift, base, slab_here, query_cols, a_ref, wo_ref
-            )
-            spread = one_hot(rel, SPAN)
-            acc_ref[:, window] += dot(grad_cell, spread, NT)
-            feats = dot(feats_ref[:, window], spread)
-            grad_kernel = (feats * cot).astype(BF16)
-            totals_ref[0:ch, 0 : hid + 16] += dot(grad_kernel, hidden, NT)
-            grad_pre = dot(wt_ref[...], grad_kernel) * slope
-            hi = grad_pre.astype(BF16)
-            low = (grad_pre - hi.astype(F32)).astype(BF16)
-            totals_ref[ch : ch + 16, 0:hid] += dot(features, hi, NT) + dot(features, low, NT)
-            return carry
-
-        return lax.fori_loop(0, blocks, block_step, carry)
-
-    lax.fori_loop(0, tiles, tile_step, 0)
-    wide = partial_ref.shape[-1]
-    for p, (x, y, h, c) in enumerate(itertools.product(range(4), range(4), range(2), range(2))):
-        first, second = ((x, y), (y, x))[c]
-        partial_ref[c, first, second, h] = acc_ref[:, p * wide : (p + 1) * wide].astype(BF16)
-
-
-def local_work(offsets, points, cot, slabs, rels, feats, w_in, b_in, w_out, b_out):
-    ch, hid = w_out.shape
-    cells = feats.shape[1]
-    tiles = slabs.shape[1] // TILE
-    vmem = pl.BlockSpec(memory_space=pltpu.VMEM)
-    smem = pl.BlockSpec(memory_space=pltpu.SMEM)
-    return pl.pallas_call(
-        compute_kernel,
-        out_shape=(
-            jax.ShapeDtypeStruct((2, 4, 4, 2, ch, cells // 64), BF16),
-            jax.ShapeDtypeStruct((ch + 16, TILE), F32),
-        ),
-        in_specs=[smem] + [vmem] * 9,
-        out_specs=(vmem, vmem),
-        scratch_shapes=[
-            pltpu.VMEM((ch, cells), F32),
-            pltpu.VMEM((tiles, KN, TILE), F32),
-            pltpu.VMEM((tiles * KN, TILE), I32),
-            pltpu.SMEM((tiles * KN, TILE), I32),
-            pltpu.VMEM((hid, 48), BF16),
-            pltpu.VMEM((ch, hid + 16), BF16),
-            pltpu.VMEM((hid, ch), BF16),
-            pltpu.SemaphoreType.DMA,
-        ],
-        compiler_params=pltpu.CompilerParams(vmem_limit_bytes=40 << 20),
-        cost_estimate=pl.CostEstimate(flops=10**9, bytes_accessed=10**7, transcendentals=0),
-        name="local_work",
-    )(offsets, points, cot, slabs, rels, feats, w_in, b_in, w_out, b_out)
+        features.append(feature)
+        preacts.append(dot(a_ref[...], jnp.concatenate([feature] * 3, 0)))
+    slopes, hiddens, kernels = [], [], []
+    for preact in preacts:
+        cdf = 0.5 + 0.5 * lax.erf(preact * math.sqrt(0.5))
+        slopes.append(cdf + preact * (jnp.exp(preact * preact * -0.5) * (1.0 / math.sqrt(2.0 * math.pi))))
+        extra = jnp.where(iota((16, preact.shape[1]), 0) < 3, 1.0, 0.0).astype(BF16)
+        hiddens.append(jnp.concatenate([(preact * cdf).astype(BF16), extra], 0))
+        kernels.append(dot(wo_ref[...], hiddens[-1]))
+    cots = [here[:ch] for here in heres]
+    grads = [(kernel * cot).astype(BF16) for kernel, cot in zip(kernels, cots)]
+    return rels, cots, features, slopes, hiddens, grads
+
+
+def entries_backward(windows, rels, cots, features, slopes, hiddens, wt_ref, totals_ref):
+    ch = cots[0].shape[0]
+    hid = slopes[0].shape[0]
+    feats = [dot(window, one_hot(rel, SPAN)) for window, rel in zip(windows, rels)]
+    grad_kernels = [(feat * cot).astype(BF16) for feat, cot in zip(feats, cots)]
+    grad_pres = [dot(wt_ref[...], g) * slope for g, slope in zip(grad_kernels, slopes)]
+    totals_ref[0:ch, 0 : hid + 16] += sum(dot(g, hidden, NT) for g, hidden in zip(grad_kernels, hiddens))
+    small = None
+    for feature, grad_pre in zip(features, grad_pres):
+        hi = grad_pre.astype(BF16)
+        low = (grad_pre - hi.astype(F32)).astype(BF16)
+        term = dot(feature, hi, NT) + dot(feature, low, NT)
+        small = term if small is None else small + term
+    totals_ref[ch : ch + 16, 0:hid] += small
 
 
 MESH_ID = pl.DeviceIdType.MESH
@@ -301,9 +230,16 @@
     pl.semaphore_wait(barrier, len(devices))
 
 
-def gather_kernel(block_ref, out_ref, send_sem, recv_sem):
+def gather_kernel(
+    offsets_ref, points_ref, cot_ref, slab_ref, rel_ref, w_in_ref, b_in_ref, w_out_ref, b_out_ref, block_ref,
+    out_ref, spread_ref, info_ref, count_ref, near_ref, cots_ref, feature_ref, slope_ref, hidden_ref,
+    a_ref, wo_ref, wt_ref,
+    send_sem, recv_sem,
+):
     me = Place()
     wide = block_ref.shape[1]
+    cells = out_ref.shape[1]
+    tiles = slab_ref.shape[1] // TILE
     sends = []
 
     def number(first, second, h, c):
@@ -336,6 +272,28 @@
             device_id_type=MESH_ID,
         ).wait_recv()
 
+    def forward(first_group, last_group):
+        def group_step(g, carry):
+            ids = [g * GROUP + n for n in range(GROUP)]
+            columns = []
+            for t in ids:
+                lanes = pl.ds(pl.multiple_of(t * TILE, TILE), TILE)
+                columns.append(query_columns(points_ref[:, lanes], cot_ref[:, lanes]))
+            infos = [jnp.concatenate([info_ref[t, 0:1, :], info_ref[t, 1:2, :]], 1) for t in ids]
+            results = entries_forward(
+                infos, [offsets_ref[0, t] for t in ids], cells, me.g, columns, a_ref, wo_ref
+            )
+            for t, rel, cot, feature, slope, hidden, grad in zip(ids, *results):
+                spread_ref[t] = dot(grad, one_hot(rel, SPAN), NT)
+                near_ref[t] = rel
+                cots_ref[t] = cot.astype(BF16)
+                feature_ref[t] = feature
+                slope_ref[t] = slope
+                hidden_ref[t] = hidden
+            return carry
+
+        lax.fori_loop(first_group, last_group, group_step, 0)
+
     steps = (1, 3, 2)
     near = [me.at(first=(me.first + n) % 4) for n in steps]
     far = [me.at(second=(me.second + n) % 4) for n in steps]
@@ -352,14 +310,21 @@
             send(spot(p), p, device)
 
     other = 1 - me.h
+    groups = tiles // GROUP
+    weight_prologue(w_in_ref, b_in_ref, w_out_ref, b_out_ref, a_ref, wo_ref, wt_ref)
+    compact(me.g, slab_ref, rel_ref, info_ref, count_ref)
     for n in steps:
         pass_on(number((me.first + n) % 4, me.second, me.h, me.c), far)
+    forward(0, groups // 4)
     pass_on(number(me.first, me.second, other, me.c), near + far)
+    forward(groups // 4, groups // 2)
     for n in steps:
         for m in (0, 1, 3, 2):
             pass_on(number((me.first + m) % 4, (me.second + n) % 4, me.h, me.c), [])
+    forward(groups // 2, groups * 3 // 4)
     for n in steps:
         pass_on(number((me.first + n) % 4, me.second, other, me.c), far)
+    forward(groups * 3 // 4, groups)
     for n in steps:
         for m in (0, 1, 3, 2):
             pass_on(number((me.first + m) % 4, (me.second + n) % 4, other, me.c), [])
@@ -371,24 +336,103 @@
         copy.wait_send()
 
 
-def gather_slab(block, owners):
+def gather_and_forward(offsets, points, cot, slabs, rels, w_in, b_in, w_out, b_out, block, owners):
     ch, wide = block.shape
+    hid = w_in.shape[0]
+    tiles = slabs.shape[1] // TILE
     vmem = pl.BlockSpec(memory_space=pltpu.VMEM)
+    smem = pl.BlockSpec(memory_space=pltpu.SMEM)
+    shape = jax.ShapeDtypeStruct
     return pl.pallas_call(
         gather_kernel,
-        out_shape=jax.ShapeDtypeStruct((ch, wide * owners), BF16),
-        in_specs=[vmem],
-        out_specs=vmem,
+        out_shape=(
+            shape((ch, wide * owners), BF16),
+            shape((tiles, ch, SPAN), F32),
+            shape((tiles, KN, TILE), F32),
+            shape((8, TILE), I32),
+            shape((tiles, 1, BLOCK), F32),
+            shape((tiles, ch, BLOCK), BF16),
+            shape((tiles, 16, BLOCK), BF16),
+            shape((tiles, hid, BLOCK), F32),
+            shape((tiles, hid + 16, BLOCK), BF16),
+            shape((hid, 48), BF16),
+            shape((ch, hid + 16), BF16),
+            shape((hid, ch), BF16),
+        ),
+        in_specs=[smem] + [vmem] * 9,
+        out_specs=(vmem,) * 12,
         scratch_shapes=[pltpu.SemaphoreType.DMA((63,)), pltpu.SemaphoreType.DMA((64,))],
         compiler_params=pltpu.CompilerParams(
-            collective_id=0, has_side_effects=True, vmem_limit_bytes=16 << 20
+            collective_id=0, has_side_effects=True, vmem_limit_bytes=40 << 20
         ),
-        name="gather_slab",
-    )(block)
+        name="gather_and_forward",
+    )(offsets, points, cot, slabs, rels, w_in, b_in, w_out, b_out, block)
+
+
+def local_kernel(
+    offsets_ref, counts_ref, points_ref, cot_ref, feats_ref, spread_ref, info_ref, a_ref, wo_ref, wt_ref,
+    partial_ref, totals_ref, window_ref,
+    acc_ref,
+):
+    slab_here = lax.axis_index("ga")
+    cells = acc_ref.shape[1]
+    tiles = spread_ref.shape[0]
+    acc_ref[...] = jnp.zeros_like(acc_ref)
+    totals_ref[...] = jnp.zeros_like(totals_ref)
+
+    def tile_step(t, carry):
+        start = offsets_ref[0, t]
+        window = pl.ds(pl.multiple_of(first_cell(start, cells), TILE), SPAN)
+        acc_ref[:, window] += spread_ref[t]
+        window_ref[t] = feats_ref[:, window]
+
+        def block_step(n, carry):
+            lanes = pl.ds(pl.multiple_of(t * TILE, TILE), TILE)
+            columns = query_columns(points_ref[:, lanes], cot_ref[:, lanes])
+            info = jnp.concatenate(
+                [info_ref[t, pl.ds(2 * n, 1), :], info_ref[t, pl.ds(2 * n + 1, 1), :]], 1
+            )
+            rels, cots, features, slopes, hiddens, grads = entries_forward(
+                [info], [start], cells, slab_here, [columns], a_ref, wo_ref
+            )
+            acc_ref[:, window] += dot(grads[0], one_hot(rels[0], SPAN), NT)
+            entries_backward(
+                [feats_ref[:, window]], rels, cots, features, slopes, hiddens, wt_ref, totals_ref
+            )
+            return carry
+
+        return lax.fori_loop(1, (counts_ref[0, t] + (BLOCK - 1)) // BLOCK, block_step, carry)
+
+    lax.fori_loop(0, tiles, tile_step, 0)
+    wide = partial_ref.shape[-1]
+    for p, (x, y, h, c) in enumerate(itertools.product(range(4), range(4), range(2), range(2))):
+        first, second = ((x, y), (y, x))[c]
+        partial_ref[c, first, second, h] = acc_ref[:, p * wide : (p + 1) * wide].astype(BF16)
+
+
+def local_sums(offsets, counts, points, cot, feats, spread, info, a, wo, wt):
+    ch, cells = feats.shape
+    vmem = pl.BlockSpec(memory_space=pltpu.VMEM)
+    smem = pl.BlockSpec(memory_space=pltpu.SMEM)
+    return pl.pallas_call(
+        local_kernel,
+        out_shape=(
+            jax.ShapeDtypeStruct((2, 4, 4, 2, ch, cells // 64), BF16),
+            jax.ShapeDtypeStruct((ch + 16, TILE), F32),
+            jax.ShapeDtypeStruct((spread.shape[0], ch, SPAN), BF16),
+        ),
+        in_specs=[smem, smem] + [vmem] * 8,
+        out_specs=(vmem, vmem, vmem),
+        scratch_shapes=[pltpu.VMEM((ch, cells), F32)],
+        compiler_params=pltpu.CompilerParams(vmem_limit_bytes=40 << 20),
+        name="local_sums",
+    )(offsets, counts, points, cot, feats, spread, info, a, wo, wt)
 
 
 def reduce_kernel(
-    partial_ref, totals_ref, out_ref, sums_ref,
+    partial_ref, beyond_ref, window_ref, near_ref, cots_ref, feature_ref, slope_ref, hidden_ref, wt_ref,
+    out_ref, sums_ref,
+    totals_ref,
     r0_ref, s0_ref, r1_ref, s1_ref, r2_ref, s2_ref, r3_ref,
     ta_ref, tf_ref, ts_ref, tz_ref, th_ref,
     sem0, sem1, sem2, sem3, tsem_a, tsem_f, tsem_s, tsem_z, tsem_h,
@@ -433,12 +477,31 @@
         + line
     )
 
+    tiles = near_ref.shape[0]
+
+    def backward(first_group, last_group):
+        def group_step(g, carry):
+            ids = [g * GROUP + n for n in range(GROUP)]
+            entries_backward(
+                [window_ref[t] for t in ids],
+                [near_ref[t] for t in ids],
+                [cots_ref[t].astype(F32) for t in ids],
+                [feature_ref[t] for t in ids],
+                [slope_ref[t] for t in ids],
+                [hidden_ref[t] for t in ids],
+                wt_ref,
+                totals_ref,
+            )
+            return carry
+
+        lax.fori_loop(first_group, last_group, group_step, 0)
+
     own_half = pl.ds(pl.multiple_of(me.c * half, 8), half)
     other_half = pl.ds(pl.multiple_of((1 - me.c) * half, 8), half)
-    send(totals_ref.at[other_half], ta_ref, tsem_a, me.sibling(), (0,), (0,))
     for n in steps + (0,):
         f = (me.second + n) % 4
         send(partial_ref.at[1 - me.c, f], r0_ref.at[f], sem0, me.sibling(), (f,), (f,))
+    totals_ref[...] = beyond_ref[...]
     for n, f in zip(steps, firsts):
         arrived(r0_ref.at[f], sem0, (f,))
         s0_ref[n - 1] = (partial_ref[me.c, f].astype(F32) + r0_ref[f].astype(F32)).astype(BF16)
@@ -446,6 +509,8 @@
             s = (me.second + m) % 4
             send(s0_ref.at[n - 1, s], r1_ref.at[3 - n, s], sem1, me.at(first=f), (3 - n, s), (n - 1, s))
 
+    backward(0, tiles // GROUP)
+    send(totals_ref.at[other_half], ta_ref, tsem_a, me.sibling(), (0,), (0,))
     arrived(ta_ref, tsem_a, (0,))
     tf_ref[me.first] = totals_ref[own_half] + ta_ref[...]
     for n, f in zip(steps, firsts):
@@ -497,7 +562,7 @@
         copy.wait_send()
 
 
-def reduce_all(partial, totals):
+def reduce_and_backward(partial, totals, windows, near, cots, feature, slope, hidden, wt):
     ch, wide = partial.shape[-2:]
     rows, lanes = totals.shape
     half = rows // 2
@@ -509,9 +574,10 @@
             jax.ShapeDtypeStruct((ch, wide), F32),
             jax.ShapeDtypeStruct((rows, lanes), F32),
         ),
-        in_specs=[vmem, vmem],
+        in_specs=[vmem] * 9,
         out_specs=(vmem, vmem),
         scratch_shapes=[
+            pltpu.VMEM((rows, lanes), F32),
             pltpu.VMEM((4, 4, 2, ch, wide), BF16),
             pltpu.VMEM((3, 4, 2, ch, wide), BF16),
             pltpu.VMEM((3, 4, 2, ch, wide), BF16),
@@ -535,19 +601,22 @@
             dma((2, 2)),
         ],
         compiler_params=pltpu.CompilerParams(
-            collective_id=1, has_side_effects=True, vmem_limit_bytes=24 << 20
+            collective_id=1, has_side_effects=True, vmem_limit_bytes=40 << 20
         ),
-        name="reduce_all",
-    )(partial, totals)
+        name="reduce_and_backward",
+    )(partial, totals, windows, near, cots, feature, slope, hidden, wt)
 
 
 def shards(query_points, cotangent, slab_ids, rel_cells, offsets, latent, w_in, b_in, w_out, b_out):
     ch, hid = w_out.shape
-    slab_feats = gather_slab(latent[0], lax.axis_size(PB))
-    partial, totals = local_work(
-        offsets, query_points, cotangent, slab_ids, rel_cells, slab_feats, w_in, b_in[None], w_out, b_out[None]
+    feats, spread, info, counts, near, cots, feature, slope, hidden, a, wo, wt = gather_and_forward(
+        offsets, query_points, cotangent, slab_ids, rel_cells,
+        w_in, b_in[None], w_out, b_out[None], latent[0], lax.axis_size(PB),
     )
-    owned, totals = reduce_all(partial, totals)
+    partial, totals, windows = local_sums(offsets, counts, query_points, cotangent, feats, spread, info, a, wo, wt)
+    owned, totals = reduce_and_backward(
+        partial, totals, windows, near, cots, feature, slope, hidden, wt
+    )
     scale = float(query_points.shape[1] * lax.axis_size(PB)) ** (-0.5)
     totals = totals * scale
     w_out_grad = totals[:ch, :hid]

time: 93.7 us -> 71.6 us (0.76)
  Pallas kernels: 88 us -> 59.5 us
  local copies, waits for them, and re-layouts: 4.04 us -> 10.4 us
    pallas_call x3, Pallas kernels: 88 us -> 59.5 us  [the longest x1 29.8 us: gather_and_forward(): pl.pallas_call(gather_kernel, out_shape=(shape((ch, wide * owners), BF16)...]
    unnamed x20, local copies, waits for them, and re-layouts: 2.22 us -> 8.53 us
where the time goes in v2:
time: 71.6 us; the launch traced here: 71.2 us
  Pallas kernels  59.5 us (83%)
  local copies, waits for them, and re-layouts  10.4 us (15%)
    pallas_call x1, Pallas kernels, gather_and_forward(): pl.pallas_call(gather_kernel, out_shape=(shape((ch, wide * owners), BF16)...  29.8 us
    pallas_call x1, Pallas kernels, reduce_and_backward(): pl.pallas_call(reduce_kernel, out_shape=(jax.ShapeDtypeStruct((ch, wide),...  27.4 us
    unnamed x20, local copies, waits for them, and re-layouts  8.53 us
    pallas_call x1, Pallas kernels, local_sums(): pl.pallas_call(local_kernel, out_shape=(jax.ShapeDtypeStruct((2, 4, 4, 2,...  2.33 us

profile of v2, /device:TPU:1, one launch (start us, length us, event | category | flops | bytes accessed | tf_op | source)
XLA Modules:
  0.0 71.2 jit_solution(4547333205020686420)
XLA Ops:
  0.6 0.8 %copy.16.w_in_ref = f32[80,6]{1,0:T(8,128)S(1)} copy(f32[80,6]{0,1:T(8,128)} %param.16) | data formatting | bytes 3840 | tf_op args[6]
  1.4 0.0 copy-start
  1.4 1.0 %copy-done = bf16[64,4096]{1,0:T(8,128)(2,1)S(1)} copy-done((bf16[64,4096]{1,0:T(8,128)(2,1)S(1)}, bf16[64,4096]{1,0:T(8,128)(2,1)}, u32[]{:S(2)}) %copy-start) | copy-done | bytes 524312
  2.5 0.0 copy-start.1
  2.5 0.8 %copy-done.1 = f32[3,4096]{1,0:T(4,128)S(1)} copy-done((f32[3,4096]{1,0:T(4,128)S(1)}, f32[3,4096]{1,0:T(4,128)}, u32[]{:S(2)}) %copy-start.1) | copy-done | bytes 49176
  3.3 0.0 copy-start.2
  3.3 0.9 %copy-done.2 = s32[8,4096]{1,0:T(8,128)S(1)} copy-done((s32[8,4096]{1,0:T(8,128)S(1)}, s32[8,4096]{1,0:T(8,128)}, u32[]{:S(2)}) %copy-start.2) | copy-done | bytes 131096
  4.2 0.0 copy-start.3
  4.2 0.9 %copy-done.3 = s32[8,4096]{1,0:T(8,128)S(1)} copy-done((s32[8,4096]{1,0:T(8,128)S(1)}, s32[8,4096]{1,0:T(8,128)}, u32[]{:S(2)}) %copy-start.3) | copy-done | bytes 131096
  5.1 0.0 copy-start.4
  5.1 0.8 %copy-done.4 = bf16[1,64,256]{2,1,0:T(8,128)(2,1)S(1)} copy-done((bf16[1,64,256]{2,1,0:T(8,128)(2,1)S(1)}, bf16[1,64,256]{2,1,0:T(8,128)(2,1)}, u32[]{:S(2)}) %copy-start.4) | copy-done | bytes 32792
  5.9 0.0 copy-start.5
  5.9 0.7 %copy-done.5 = bf16[64,80]{1,0:T(8,128)(2,1)S(1)} copy-done((bf16[64,80]{1,0:T(8,128)(2,1)S(1)}, bf16[64,80]{1,0:T(8,128)(2,1)}, u32[]{:S(2)}) %copy-start.5) | copy-done | bytes 10264
  6.6 0.0 copy-start.6
  6.6 0.7 copy-done.6
  7.2 0.0 copy-start.7
  7.2 0.7 copy-done.7
  7.9 0.0 copy-start.8
  7.9 0.7 copy-done.8
  8.5 29.8 %gather_and_forward.1 = (bf16[64,16384]{1,0:T(8,128)(2,1)S(1)}, f32[32,64,640]{2,1,0:T(8,128)S(1)}, f32[32,8,128]{2,1,0:T(8,128)S(1)}, s32[8,128]{1,0:T(8,128)S(...) custom-call(s32[1,32]{1,0:T(1,128)S(1)} %copy-done.6, ...), custom_call_target="tpu_custom_call" | custom-call | tf_op jit(solution)/shard_map/gather_and_forward/pallas_call | solution.py:346
  38.4 2.3 %local_sums.1 = (bf16[2,4,4,2,64,256]{5,4,3,2,1,0:T(8,128)(2,1)S(1)}, f32[80,128]{1,0:T(8,128)S(1)}, bf16[32,64,640]{2,1,0:T(8,128)(2,1)S(1)}) custom-call(s32[1,32]{1,0:T(1,128)S(1)} %copy-done.6, s32[8,128]{1,0:T(8,128)S(1)} %get-tuple-element.22.counts_ref, f32[3,4096]{1,0:T(4,128)S(1)} %copy-done.1, bf16[64,4096]{1,0:T(8,128)(2,1)S(1)} %copy-done, ...), custom_call_target="tpu_custom_call" | custom-call | tf_op jit(solution)/shard_map/local_sums/pallas_call | solution.py:417
  40.7 27.4 %reduce_and_backward.1 = (f32[64,256]{1,0:T(8,128)S(1)}, f32[80,128]{1,0:T(8,128)S(1)}) custom-call(bf16[2,4,4,2,64,256]{5,4,3,2,1,0:T(8,128)(2,1)S(1)} %get-tuple-element.29.partial_ref, f32[80,128]{1,0:T(8,128)S(1)} %get-tuple-element.30.beyond_ref, bf16[32,64,640]{2,1,0:T(8,128)(2,1)S(1)} %get-tuple-element.31.window_ref, ...), custom_call_target="tpu_custom_call" | custom-call | tf_op jit(solution)/shard_map/reduce_and_backward/pallas_call | solution.py:571
  68.1 0.5 slice_bitcast_fusion
  68.6 0.7 slice_reduce_fusion
  69.3 0.6 slice.39
  69.9 0.6 maximum_bitcast_fusion
  70.5 0.6 copy.18
  (2 shorter events, 0.0 us)
Async XLA Ops:
  1.4 1.0 %copy-start = (bf16[64,4096]{1,0:T(8,128)(2,1)S(1)}, bf16[64,4096]{1,0:T(8,128)(2,1)}, u32[]{:S(2)}) copy-start(bf16[64,4096]{1,0:T(8,128)(2,1)} %cot_ref.3) | copy-start | bytes 1572868
  2.5 0.8 %copy-start.1 = (f32[3,4096]{1,0:T(4,128)S(1)}, f32[3,4096]{1,0:T(4,128)}, u32[]{:S(2)}) copy-start(f32[3,4096]{1,0:T(4,128)} %points_ref.3) | copy-start | bytes 147460
  3.3 0.9 %copy-start.2 = (s32[8,4096]{1,0:T(8,128)S(1)}, s32[8,4096]{1,0:T(8,128)}, u32[]{:S(2)}) copy-start(s32[8,4096]{1,0:T(8,128)} %slab_ref.1) | copy-start | bytes 393220
  4.2 0.9 %copy-start.3 = (s32[8,4096]{1,0:T(8,128)S(1)}, s32[8,4096]{1,0:T(8,128)}, u32[]{:S(2)}) copy-start(s32[8,4096]{1,0:T(8,128)} %rel_ref.1) | copy-start | bytes 393220
  5.1 0.8 %copy-start.4 = (bf16[1,64,256]{2,1,0:T(8,128)(2,1)S(1)}, bf16[1,64,256]{2,1,0:T(8,128)(2,1)}, u32[]{:S(2)}) copy-start(bf16[1,64,256]{2,1,0:T(8,128)(2,1)} %param.15) | copy-start | bytes 98308
  5.9 0.7 %copy-start.5 = (bf16[64,80]{1,0:T(8,128)(2,1)S(1)}, bf16[64,80]{1,0:T(8,128)(2,1)}, u32[]{:S(2)}) copy-start(bf16[64,80]{1,0:T(8,128)(2,1)} %w_out_ref.1) | copy-start | bytes 30724
  6.6 0.7 copy-start.6
  7.2 0.7 copy-start.7
  7.9 0.7 copy-start.8

commit v3 on v2

--- a/solution.py
+++ b/solution.py
@@ -52,32 +52,28 @@
 
 
 def weight_prologue(w_in_ref, b_in_ref, w_out_ref, b_out_ref, a_ref, wo_ref, wt_ref):
-    hid = w_in_ref.shape[0]
+    hid = w_in_ref.shape[1]
     ch = w_out_ref.shape[0]
-    parts = split3(w_in_ref[...])
-    bias = split3(b_in_ref[...])
-    total = jnp.zeros((hid, 48), F32)
-    for n in range(3):
+    total = jnp.zeros((48, hid), F32)
+    row = iota((48, hid), 0)
+    for n, (weight, bias) in enumerate(zip(split3(w_in_ref[...]), split3(b_in_ref[...]))):
         place = unit(
-            (6, 48),
-            lambda r, c, n=n: (c // 16 == n)
+            (48, 6),
+            lambda c, r, n=n: (c // 16 == n)
             & (((r < 3) & (c % 16 < 9) & (c % 16 % 3 == r)) | ((r >= 3) & (c % 16 == r + 6))),
         )
-        total += dot(parts[n], place)
+        total += dot(place, weight)
+        total += jnp.where(row == 16 * n + 12, bias.astype(F32), 0.0)
+    same = unit((hid, hid), lambda r, c: r == c)
+    a_ref[...] = dot(same, total.astype(BF16), NT).astype(BF16)
+    wt_ref[...] = dot(same, w_out_ref[...], NT).astype(BF16)
+    total = dot(w_out_ref[...], unit((hid, hid + 16), lambda r, c: r == c))
+    for n, bias in enumerate(split3(b_out_ref[...])):
         diag = jnp.where(
-            iota((hid, hid), 0) == iota((hid, hid), 1), jnp.broadcast_to(bias[n].astype(F32), (hid, hid)), 0.0
-        ).astype(BF16)
-        total += dot(diag, unit((hid, 48), lambda r, c, n=n: c == 16 * n + 12))
-    a_ref[...] = total.astype(BF16)
-    bias = split3(b_out_ref[...])
-    total = dot(w_out_ref[...], unit((hid, hid + 16), lambda r, c: r == c))
-    for n in range(3):
-        diag = jnp.where(
-            iota((ch, ch), 0) == iota((ch, ch), 1), jnp.broadcast_to(bias[n].astype(F32), (ch, ch)), 0.0
+            iota((ch, ch), 0) == iota((ch, ch), 1), jnp.broadcast_to(bias.astype(F32), (ch, ch)), 0.0
         ).astype(BF16)
         total += dot(diag, unit((ch, hid + 16), lambda r, c, n=n: c == hid + n))
     wo_ref[...] = total.astype(BF16)
-    wt_ref[...] = dot(unit((hid, hid), lambda r, c: r == c), w_out_ref[...], NT).astype(BF16)
 
 
 def compact(slab_here, slab_ref, rel_ref, info_ref, count_ref):
@@ -227,16 +223,31 @@
     barrier = pltpu.get_barrier_semaphore()
     for device in devices:
         pl.semaphore_signal(barrier, inc=1, device_id=device, device_id_type=MESH_ID)
-    pl.semaphore_wait(barrier, len(devices))
+    return lambda: pl.semaphore_wait(barrier, len(devices))
+
+
+def load_all(pairs, sems):
+    copies = [
+        pltpu.make_async_copy(source, target, sems.at[n]) for n, (source, target) in enumerate(pairs)
+    ]
+    for copy in copies:
+        copy.start()
+    return copies
 
 
 def gather_kernel(
-    offsets_ref, points_ref, cot_ref, slab_ref, rel_ref, w_in_ref, b_in_ref, w_out_ref, b_out_ref, block_ref,
+    *refs,
+):
+    sources = refs[:10]
+    targets = refs[22:32]
+    offsets_ref, points_ref, cot_ref, slab_ref, rel_ref, w_in_ref, b_in_ref, w_out_ref, b_out_ref, block_ref = targets
+    (
     out_ref, spread_ref, info_ref, count_ref, near_ref, cots_ref, feature_ref, slope_ref, hidden_ref,
     a_ref, wo_ref, wt_ref,
-    send_sem, recv_sem,
-):
+    ) = refs[10:22]
+    load_sem, send_sem, recv_sem = refs[32:]
     me = Place()
+    loads = load_all(list(zip(sources, targets)), load_sem)
     wide = block_ref.shape[1]
     cells = out_ref.shape[1]
     tiles = slab_ref.shape[1] // TILE
@@ -298,8 +309,14 @@
     near = [me.at(first=(me.first + n) % 4) for n in steps]
     far = [me.at(second=(me.second + n) % 4) for n in steps]
     across = me.at(h=1 - me.h)
-    greet([me.sibling(), across] + near + far)
+    all_here = greet([me.sibling(), across] + near + far)
     mine = number(me.first, me.second, me.h, me.c)
+    groups = tiles // GROUP
+    for copy in loads:
+        copy.wait()
+    weight_prologue(w_in_ref, b_in_ref, w_out_ref, b_out_ref, a_ref, wo_ref, wt_ref)
+    compact(me.g, slab_ref, rel_ref, info_ref, count_ref)
+    all_here()
     for device in [across] + near + far + [me.sibling()]:
         send(block_ref, mine, device)
     out_ref[:, pl.ds(pl.multiple_of(mine * wide, wide), wide)] = block_ref[...]
@@ -310,21 +327,16 @@
             send(spot(p), p, device)
 
     other = 1 - me.h
-    groups = tiles // GROUP
-    weight_prologue(w_in_ref, b_in_ref, w_out_ref, b_out_ref, a_ref, wo_ref, wt_ref)
-    compact(me.g, slab_ref, rel_ref, info_ref, count_ref)
+    forward(0, groups // 2)
     for n in steps:
         pass_on(number((me.first + n) % 4, me.second, me.h, me.c), far)
-    forward(0, groups // 4)
+    forward(groups // 2, groups)
     pass_on(number(me.first, me.second, other, me.c), near + far)
-    forward(groups // 4, groups // 2)
     for n in steps:
         for m in (0, 1, 3, 2):
             pass_on(number((me.first + m) % 4, (me.second + n) % 4, me.h, me.c), [])
-    forward(groups // 2, groups * 3 // 4)
     for n in steps:
         pass_on(number((me.first + n) % 4, me.second, other, me.c), far)
-    forward(groups * 3 // 4, groups)
     for n in steps:
         for m in (0, 1, 3, 2):
             pass_on(number((me.first + m) % 4, (me.second + n) % 4, other, me.c), [])
@@ -338,10 +350,9 @@
 
 def gather_and_forward(offsets, points, cot, slabs, rels, w_in, b_in, w_out, b_out, block, owners):
     ch, wide = block.shape
-    hid = w_in.shape[0]
+    hid = w_in.shape[1]
     tiles = slabs.shape[1] // TILE
     vmem = pl.BlockSpec(memory_space=pltpu.VMEM)
-    smem = pl.BlockSpec(memory_space=pltpu.SMEM)
     shape = jax.ShapeDtypeStruct
     return pl.pallas_call(
         gather_kernel,
@@ -359,9 +370,14 @@
             shape((ch, hid + 16), BF16),
             shape((hid, ch), BF16),
         ),
-        in_specs=[smem] + [vmem] * 9,
+        in_specs=[pl.BlockSpec(memory_space=pltpu.HBM)] * 10,
         out_specs=(vmem,) * 12,
-        scratch_shapes=[pltpu.SemaphoreType.DMA((63,)), pltpu.SemaphoreType.DMA((64,))],
+        scratch_shapes=[pltpu.SMEM(offsets.shape, I32)]
+        + [
+            pltpu.VMEM(value.shape, value.dtype)
+            for value in (points, cot, slabs, rels, w_in, b_in, w_out, b_out, block)
+        ]
+        + [pltpu.SemaphoreType.DMA((n,)) for n in (10, 63, 64)],
         compiler_params=pltpu.CompilerParams(
             collective_id=0, has_side_effects=True, vmem_limit_bytes=40 << 20
         ),
@@ -370,15 +386,17 @@
 
 
 def local_kernel(
-    offsets_ref, counts_ref, points_ref, cot_ref, feats_ref, spread_ref, info_ref, a_ref, wo_ref, wt_ref,
+    counts_ref, offsets_hbm, points_ref, cot_ref, feats_ref, spread_ref, info_ref, a_ref, wo_ref, wt_ref,
     partial_ref, totals_ref, window_ref,
-    acc_ref,
+    acc_ref, offsets_ref, some_points_ref, some_cot_ref, sem,
 ):
     slab_here = lax.axis_index("ga")
     cells = acc_ref.shape[1]
     tiles = spread_ref.shape[0]
+    (load,) = load_all([(offsets_hbm, offsets_ref)], sem)
     acc_ref[...] = jnp.zeros_like(acc_ref)
     totals_ref[...] = jnp.zeros_like(totals_ref)
+    load.wait()
 
     def tile_step(t, carry):
         start = offsets_ref[0, t]
@@ -388,7 +406,11 @@
 
         def block_step(n, carry):
             lanes = pl.ds(pl.multiple_of(t * TILE, TILE), TILE)
-            columns = query_columns(points_ref[:, lanes], cot_ref[:, lanes])
+            for copy in load_all(
+                [(points_ref.at[:, lanes], some_points_ref), (cot_ref.at[:, lanes], some_cot_ref)], sem
+            ):
+                copy.wait()
+            columns = query_columns(some_points_ref[...], some_cot_ref[...])
             info = jnp.concatenate(
                 [info_ref[t, pl.ds(2 * n, 1), :], info_ref[t, pl.ds(2 * n + 1, 1), :]], 1
             )
@@ -413,7 +435,6 @@
 def local_sums(offsets, counts, points, cot, feats, spread, info, a, wo, wt):
     ch, cells = feats.shape
     vmem = pl.BlockSpec(memory_space=pltpu.VMEM)
-    smem = pl.BlockSpec(memory_space=pltpu.SMEM)
     return pl.pallas_call(
         local_kernel,
         out_shape=(
@@ -421,12 +442,18 @@
             jax.ShapeDtypeStruct((ch + 16, TILE), F32),
             jax.ShapeDtypeStruct((spread.shape[0], ch, SPAN), BF16),
         ),
-        in_specs=[smem, smem] + [vmem] * 8,
+        in_specs=[pl.BlockSpec(memory_space=pltpu.SMEM)] + [pl.BlockSpec(memory_space=pltpu.HBM)] * 3 + [vmem] * 6,
         out_specs=(vmem, vmem, vmem),
-        scratch_shapes=[pltpu.VMEM((ch, cells), F32)],
+        scratch_shapes=[
+            pltpu.VMEM((ch, cells), F32),
+            pltpu.SMEM(offsets.shape, I32),
+            pltpu.VMEM((points.shape[0], TILE), F32),
+            pltpu.VMEM((ch, TILE), BF16),
+            pltpu.SemaphoreType.DMA((2,)),
+        ],
         compiler_params=pltpu.CompilerParams(vmem_limit_bytes=40 << 20),
         name="local_sums",
-    )(offsets, counts, points, cot, feats, spread, info, a, wo, wt)
+    )(counts, offsets, points, cot, feats, spread, info, a, wo, wt)
 
 
 def reduce_kernel(
@@ -470,7 +497,7 @@
     depths = [(depth + n) % 8 for n in range(1, 8)]
     line = [me.at(h=d // 4, g=d % 4) for d in depths]
     across = me.at(h=1 - me.h)
-    greet(
+    all_here = greet(
         [me.sibling()]
         + [me.at(first=f) for f in firsts]
         + [me.at(second=s) for s in seconds]
@@ -498,27 +525,27 @@
 
     own_half = pl.ds(pl.multiple_of(me.c * half, 8), half)
     other_half = pl.ds(pl.multiple_of((1 - me.c) * half, 8), half)
-    for n in steps + (0,):
-        f = (me.second + n) % 4
-        send(partial_ref.at[1 - me.c, f], r0_ref.at[f], sem0, me.sibling(), (f,), (f,))
     totals_ref[...] = beyond_ref[...]
-    for n, f in zip(steps, firsts):
-        arrived(r0_ref.at[f], sem0, (f,))
-        s0_ref[n - 1] = (partial_ref[me.c, f].astype(F32) + r0_ref[f].astype(F32)).astype(BF16)
-        for m in steps + (0,):
-            s = (me.second + m) % 4
+    backward(0, tiles // GROUP)
+    all_here()
+    send(totals_ref.at[other_half], ta_ref, tsem_a, me.sibling(), (0,), (0,))
+    for m in steps + (0,):
+        for n in steps + (0,):
+            f, s = (me.second + n) % 4, (me.first + m) % 4
+            send(partial_ref.at[1 - me.c, f, s], r0_ref.at[f, s], sem0, me.sibling(), (f, s), (f, s))
+    for m in steps + (0,):
+        s = (me.second + m) % 4
+        for n, f in zip(steps, firsts):
+            arrived(r0_ref.at[f, s], sem0, (f, s))
+            s0_ref[n - 1, s] = (partial_ref[me.c, f, s].astype(F32) + r0_ref[f, s].astype(F32)).astype(BF16)
             send(s0_ref.at[n - 1, s], r1_ref.at[3 - n, s], sem1, me.at(first=f), (3 - n, s), (n - 1, s))
-
-    backward(0, tiles // GROUP)
-    send(totals_ref.at[other_half], ta_ref, tsem_a, me.sibling(), (0,), (0,))
     arrived(ta_ref, tsem_a, (0,))
     tf_ref[me.first] = totals_ref[own_half] + ta_ref[...]
     for n, f in zip(steps, firsts):
         send(tf_ref.at[me.first], tf_ref.at[me.first], tsem_f, me.at(first=f), (me.first,), (n,))
 
-    arrived(r0_ref.at[me.first], sem0, (me.first,))
-
     def collect(s):
+        arrived(r0_ref.at[me.first, s], sem0, (me.first, s))
         total = partial_ref[me.c, me.first, s].astype(F32) + r0_ref[me.first, s].astype(F32)
         for n in range(3):
             arrived(r1_ref.at[n, s], sem1, (n, s))
@@ -590,7 +617,7 @@
             pltpu.VMEM((4, half, lanes), F32),
             pltpu.VMEM((8, half, lanes), F32),
             pltpu.VMEM((2, half, lanes), F32),
-            dma((2, 4)),
+            dma((2, 4, 4)),
             dma((2, 3, 4)),
             dma((2, 3)),
             dma((2, 1)),
@@ -607,24 +634,54 @@
     )(partial, totals, windows, near, cots, feature, slope, hidden, wt)
 
 
+def final_kernel(scale, owned_ref, sums_ref, grid_ref, w_in_ref, b_in_ref, w_out_ref, b_out_ref, sem):
+    copy = pltpu.make_async_copy(owned_ref, grid_ref, sem)
+    copy.start()
+    ch, hid = w_out_ref.shape
+    outer = sums_ref[0:ch] * scale
+    rows = sums_ref[ch : ch + 16, 0:hid] * scale
+    w_out_ref[...] = outer[:, 0:hid]
+    turned = jnp.concatenate([outer, jnp.zeros((TILE - ch, TILE), F32)], 0).T
+    b_out_ref[...] = turned[hid : hid + 1, 0:ch]
+    w_in_ref[...] = jnp.concatenate([rows[0:3] + rows[3:6] + rows[6:9], rows[9:12]], 0)
+    b_in_ref[...] = rows[12:13]
+    copy.wait()
+
+
+def final_form(owned, sums, scale, hid):
+    ch = owned.shape[0]
+    vmem = pl.BlockSpec(memory_space=pltpu.VMEM)
+    shape = jax.ShapeDtypeStruct
+    return pl.pallas_call(
+        functools.partial(final_kernel, scale),
+        out_shape=(
+            shape(owned.shape, F32),
+            shape((6, hid), F32),
+            shape((1, hid), F32),
+            shape((ch, hid), F32),
+            shape((1, ch), F32),
+        ),
+        in_specs=[vmem, vmem],
+        out_specs=(pl.BlockSpec(memory_space=pltpu.HBM),) + (vmem,) * 4,
+        scratch_shapes=[pltpu.SemaphoreType.DMA],
+        name="final_form",
+    )(owned, sums)
+
+
 def shards(query_points, cotangent, slab_ids, rel_cells, offsets, latent, w_in, b_in, w_out, b_out):
-    ch, hid = w_out.shape
     feats, spread, info, counts, near, cots, feature, slope, hidden, a, wo, wt = gather_and_forward(
         offsets, query_points, cotangent, slab_ids, rel_cells,
-        w_in, b_in[None], w_out, b_out[None], latent[0], lax.axis_size(PB),
+        w_in.T, b_in[None], w_out, b_out[None], latent[0], lax.axis_size(PB),
     )
-    partial, totals, windows = local_sums(offsets, counts, query_points, cotangent, feats, spread, info, a, wo, wt)
+    partial, totals, windows = local_sums(
+        offsets, counts, query_points, cotangent, feats, spread, info, a, wo, wt
+    )
     owned, totals = reduce_and_backward(
         partial, totals, windows, near, cots, feature, slope, hidden, wt
     )
     scale = float(query_points.shape[1] * lax.axis_size(PB)) ** (-0.5)
-    totals = totals * scale
-    w_out_grad = totals[:ch, :hid]
-    b_out_grad = totals[:ch, hid]
-    rows = totals[ch:, :hid]
-    w_in_grad = jnp.concatenate([rows[0:3] + rows[3:6] + rows[6:9], rows[9:12]], 0).T
-    b_in_grad = rows[12]
-    return owned[None], w_in_grad, b_in_grad, w_out_grad, b_out_grad
+    grid, w_in_grad, b_in_grad, w_out_grad, b_out_grad = final_form(owned, totals, scale, w_out.shape[1])
+    return grid[None], w_in_grad.T, b_in_grad[0], w_out_grad, b_out_grad[0]
 
 
 def solution(mesh):

time: 71.6 us -> 72.9 us (1.018)
  Pallas kernels: 59.5 us -> 62.8 us
  local copies, waits for them, and re-layouts: 10.4 us -> 9.03 us
    pallas_call x0 -> x1, Pallas kernels: none -> 2.1 us  [final_form(): pl.pallas_call(functools.partial(final_kernel, scale), out_shape=(shape(o...]
    slice x2 -> x0, local copies, waits for them, and re-layouts: 1.31 us -> none  [the longest x1 0.69 us: shards(): b_out_grad = totals[:ch, hid]]
    unnamed x20 -> x24, local copies, waits for them, and re-layouts: 8.53 us -> 9.03 us
where the time goes in v3:
time: 72.9 us; the launch traced here: 72.5 us
  Pallas kernels  62.8 us (86%)
  local copies, waits for them, and re-layouts  9.03 us (12%)
    pallas_call x1, Pallas kernels, gather_and_forward(): pl.pallas_call(gather_kernel, out_shape=(shape((ch, wide * owners), BF16)...  30.3 us
    pallas_call x1, Pallas kernels, reduce_and_backward(): pl.pallas_call(reduce_kernel, out_shape=(jax.ShapeDtypeStruct((ch, wide),...  27.8 us
    unnamed x24, local copies, waits for them, and re-layouts  9.03 us
    pallas_call x1, Pallas kernels, local_sums(): pl.pallas_call(local_kernel, out_shape=(jax.ShapeDtypeStruct((2, 4, 4, 2,...  2.61 us
    pallas_call x1, Pallas kernels, final_form(): pl.pallas_call(functools.partial(final_kernel, scale), out_shape=(shape(o...  2.1 us

profile of v3, /device:TPU:1, one launch (start us, length us, event | category | flops | bytes accessed | tf_op | source)
XLA Modules:
  0.0 72.5 jit_solution(11181423625702550953)
XLA Ops:
  0.6 0.0 copy-start
  0.6 1.0 %copy-done = bf16[64,4096]{1,0:T(8,128)(2,1)S(1)} copy-done((bf16[64,4096]{1,0:T(8,128)(2,1)S(1)}, bf16[64,4096]{1,0:T(8,128)(2,1)}, u32[]{:S(2)}) %copy-start) | copy-done | bytes 524312
  1.7 0.0 copy-start.1
  1.7 0.8 %copy-done.1 = f32[3,4096]{1,0:T(4,128)S(1)} copy-done((f32[3,4096]{1,0:T(4,128)S(1)}, f32[3,4096]{1,0:T(4,128)}, u32[]{:S(2)}) %copy-start.1) | copy-done | bytes 49176
  2.5 0.0 copy-start.2
  2.5 0.9 %copy-done.2 = s32[8,4096]{1,0:T(8,128)S(1)} copy-done((s32[8,4096]{1,0:T(8,128)S(1)}, s32[8,4096]{1,0:T(8,128)}, u32[]{:S(2)}) %copy-start.2) | copy-done | bytes 131096
  3.4 0.0 copy-start.3
  3.4 0.9 %copy-done.3 = s32[8,4096]{1,0:T(8,128)S(1)} copy-done((s32[8,4096]{1,0:T(8,128)S(1)}, s32[8,4096]{1,0:T(8,128)}, u32[]{:S(2)}) %copy-start.3) | copy-done | bytes 131096
  4.3 0.0 copy-start.6
  4.3 0.8 %copy-done.6 = bf16[1,64,256]{2,1,0:T(8,128)(2,1)S(1)} copy-done((bf16[1,64,256]{2,1,0:T(8,128)(2,1)S(1)}, bf16[1,64,256]{2,1,0:T(8,128)(2,1)}, u32[]{:S(2)}) %copy-start.6) | copy-done | bytes 32792
  5.1 0.0 copy-start.7
  5.1 0.7 copy-done.7
  5.8 0.0 copy-start.8
  5.8 0.7 copy-done.8
  6.5 0.0 copy-start.9
  6.5 0.7 copy-done.9
  7.1 0.0 copy-start.10
  7.1 0.7 copy-done.10
  7.8 0.0 copy-start.11
  7.8 0.7 copy-done.11
  8.5 30.3 %gather_and_forward.1 = (bf16[64,16384]{1,0:T(8,128)(2,1)S(1)}, f32[32,64,640]{2,1,0:T(8,128)S(1)}, f32[32,8,128]{2,1,0:T(8,128)S(1)}, s32[8,128]{1,0:T(8,128)S(...) custom-call(s32[1,32]{1,0:T(1,128)S(1)} %copy-done.9, ...), custom_call_target="tpu_custom_call" | custom-call | tf_op jit(solution)/shard_map/gather_and_forward/pallas_call | solution.py:357
  38.7 2.6 %local_sums.1 = (bf16[2,4,4,2,64,256]{5,4,3,2,1,0:T(8,128)(2,1)S(1)}, f32[80,128]{1,0:T(8,128)S(1)}, bf16[32,64,640]{2,1,0:T(8,128)(2,1)S(1)}) custom-call(s32[8,128]{1,0:T(8,128)S(1)} %get-tuple-element.27.counts_ref, s32[1,32]{1,0:T(1,128)S(1)} %copy-done.9, f32[3,4096]{1,0:T(4,128)S(1)} %copy-done.1, bf16[64,4096]{1,0:T(8,128)(2,1)S(1)} %copy-done, ...), custom_call_target="tpu_custom_call" | custom-call | tf_op jit(solution)/shard_map/local_sums/pallas_call | solution.py:438
  41.3 27.8 %reduce_and_backward.1 = (f32[64,256]{1,0:T(8,128)S(1)}, f32[80,128]{1,0:T(8,128)S(1)}) custom-call(bf16[2,4,4,2,64,256]{5,4,3,2,1,0:T(8,128)(2,1)S(1)} %get-tuple-element.34.partial_ref, f32[80,128]{1,0:T(8,128)S(1)} %get-tuple-element.35.beyond_ref, bf16[32,64,640]{2,1,0:T(8,128)(2,1)S(1)} %get-tuple-element.36.window_ref, ...), custom_call_target="tpu_custom_call" | custom-call | tf_op jit(solution)/shard_map/reduce_and_backward/pallas_call | solution.py:598
  69.2 0.0 copy-start.4
  69.2 0.6 copy-done.4
  69.8 0.0 copy-start.5
  69.8 0.6 copy-done.5
  70.4 2.1 %final_form.1 = (f32[64,256]{1,0:T(8,128)}, f32[6,80]{1,0:T(8,128)}, f32[1,80]{1,0:T(1,128)}, f32[64,80]{1,0:T(8,128)}, f32[1,64]{1,0:T(1,128)}) custom-call(f32[64,256]{1,0:T(8,128)} %copy-done.4, f32[80,128]{1,0:T(8,128)} %copy-done.5), custom_call_target="tpu_custom_call" | custom-call | tf_op jit(solution)/shard_map/final_form/pallas_call | solution.py:655
Async XLA Ops:
  0.6 1.0 %copy-start = (bf16[64,4096]{1,0:T(8,128)(2,1)S(1)}, bf16[64,4096]{1,0:T(8,128)(2,1)}, u32[]{:S(2)}) copy-start(bf16[64,4096]{1,0:T(8,128)(2,1)} %cot_ref.1) | copy-start | bytes 1572868
  1.7 0.8 %copy-start.1 = (f32[3,4096]{1,0:T(4,128)S(1)}, f32[3,4096]{1,0:T(4,128)}, u32[]{:S(2)}) copy-start(f32[3,4096]{1,0:T(4,128)} %points_ref.1) | copy-start | bytes 147460
  2.5 0.9 %copy-start.2 = (s32[8,4096]{1,0:T(8,128)S(1)}, s32[8,4096]{1,0:T(8,128)}, u32[]{:S(2)}) copy-start(s32[8,4096]{1,0:T(8,128)} %refs_3_.1) | copy-start | bytes 393220
  3.4 0.9 %copy-start.3 = (s32[8,4096]{1,0:T(8,128)S(1)}, s32[8,4096]{1,0:T(8,128)}, u32[]{:S(2)}) copy-start(s32[8,4096]{1,0:T(8,128)} %refs_4_.1) | copy-start | bytes 393220
  4.3 0.8 %copy-start.6 = (bf16[1,64,256]{2,1,0:T(8,128)(2,1)S(1)}, bf16[1,64,256]{2,1,0:T(8,128)(2,1)}, u32[]{:S(2)}) copy-start(bf16[1,64,256]{2,1,0:T(8,128)(2,1)} %param.15) | copy-start | bytes 98308
  5.1 0.7 copy-start.7
  5.8 0.7 copy-start.8
  6.5 0.7 copy-start.9
  7.1 0.7 copy-start.10
  7.8 0.7 copy-start.11
  69.2 0.6 copy-start.4
  69.8 0.6 copy-start.5
